TPU v7x, 32 devices: a whole 2x2x4 slice. The times are simulated.
32 devices in a mesh: gx: 4 (over x, core), gy: 8 (over z, y).
Axes of the slice: x: 2, y: 2, z: 4, core: 2. Of those that a mesh axis runs over, the one named last changes fastest.
Arguments:
- fine_source: bfloat16 [4, 8, 4, 8000], P('gx', 'gy'), may hold values from -6 to 6
- fine_blocks: bfloat16 [3, 12, 20, 20], replicated, may hold values from -0.5 to 0.5
- coarse_blocks: bfloat16 [3, 12, 20, 20], replicated, may hold values from -0.5 to 0.5
- child_filter_matrices: bfloat16 [2, 20, 20], replicated, may hold values from -1 to 1
Outputs:
- fine_result: float32 [4, 8, 4, 8000], P('gx', 'gy')
All inputs are finite; a program needn't handle non-finite values.
Results may differ from a plain program's by a relative error of at most 0.013.
Values may be sent and summed in bfloat16 or wider, within the bound.
A program may use at most 64 MiB of HBM per device.

v0:
```python
import functools

import jax
import jax.numpy as jnp
from jax import lax
from jax.experimental import pallas as pl
from jax.experimental.pallas import tpu as pltpu
from jax.sharding import PartitionSpec as P

BF = jnp.bfloat16
F32 = jnp.float32
PAIR = 2
SUB = 32
LANES = 128


def shifted(block, axis, distance):
    devices = range(lax.axis_size(axis))
    route = [(i - distance, i) for i in devices if i - distance in devices]
    return lax.ppermute(block, axis, route)


def partner(block, axis):
    count = lax.axis_size(axis)
    return lax.ppermute(block, axis, [(i, i ^ 1) for i in range(count)])


TROW = 24


def spread(rows, boxes, n):
    r = lax.broadcasted_iota(jnp.int32, (rows, LANES), 0)
    c = lax.broadcasted_iota(jnp.int32, (rows, LANES), 1)
    return jnp.where((lax.rem(c, n) == r) & (c < boxes * n), 1.0, 0.0).astype(BF)


def spread_t(cols, boxes, n):
    r = lax.broadcasted_iota(jnp.int32, (LANES, cols), 0)
    c = lax.broadcasted_iota(jnp.int32, (LANES, cols), 1)
    return jnp.where((lax.rem(r, n) == c) & (r < boxes * n), 1.0, 0.0).astype(BF)


def box_of(n):
    r = lax.broadcasted_iota(jnp.int32, (LANES, LANES), 0)
    c = lax.broadcasted_iota(jnp.int32, (LANES, LANES), 1)
    return lax.div(r, n), lax.div(c, n)


def tiled(padded, pieces, boxes_in, boxes_out, n):
    wide = dot(padded[:, :SUB].astype(BF), spread(SUB, boxes_in, n)).astype(BF)
    left = spread_t(TROW, boxes_out, n)
    return [dot(left, wide[p * TROW : (p + 1) * TROW]) for p in range(pieces)]


def level_mats(blk, pad, first, second, third, boxes):
    count, n, _ = blk.shape
    terms = count // 3
    pad[...] = jnp.zeros_like(pad)
    second[...] = jnp.zeros_like(second)
    for p in range(count):
        pad[p * TROW : p * TROW + n, :n] = blk[p].astype(F32)
    zero = jnp.zeros((TROW, LANES), F32)
    row, col = box_of(n)
    wide = tiled(pad[...], count, boxes, boxes, n)
    for m in range(terms):
        g, f = divmod(m, PAIR)
        low, mid, up = (pad[(e * terms + m) * TROW : (e * terms + m + 1) * TROW, :] for e in range(3))
        main = mid + pltpu.roll(up, SUB, 1) + pltpu.roll(low, 2 * SUB, 1)
        third_slot = pltpu.roll(mid, 3 * SUB, 1)
        at = f * 4 * TROW
        for t, (x, y) in enumerate([(main, zero), (third_slot, zero), (zero, mid), (mid, zero)]):
            first[g, at + t * TROW : at + (t + 1) * TROW, :LANES] = x
            first[g, at + t * TROW : at + (t + 1) * TROW, LANES:] = y
        at = f * 2 * SUB
        second[g, at : at + TROW, f * LANES : (f + 1) * LANES] = main
        second[g, at + SUB : at + SUB + TROW, f * LANES : (f + 1) * LANES] = third_slot
        at = m * 2 * LANES
        third[:, at : at + LANES] = jnp.where(row == col, wide[terms + m], 0.0).astype(BF)
        third[:, at + LANES : at + 2 * LANES] = (
            jnp.where(col == row + 1, wide[2 * terms + m], 0.0)
            + jnp.where(col == row - 1, wide[m], 0.0)
        ).astype(BF)


def pair_mats(mats, pad, boxes_in, boxes_out, n):
    row, col = box_of(n)
    fine, parent = (col, row) if boxes_in > boxes_out else (row, col)
    for c in range(2):
        pad[c * TROW : c * TROW + n, :n] = mats[c].astype(F32)
    wide = tiled(pad[: 2 * TROW, :], 2, boxes_in, boxes_out, n)
    keep = lax.div(fine, 2) == parent
    even = lax.rem(fine, 2) == 0
    return jnp.where(keep, jnp.where(even, wide[0], wide[1]), 0.0).astype(BF)


def small(mat, pad, at):
    n = mat.shape[0]
    pad[at * SUB : at * SUB + n, :n] = mat.astype(F32)
    return pad[at * SUB : (at + 1) * SUB, :SUB].astype(BF)


def dot_t(a, b):
    return lax.dot_general(a, b, (((1,), (1,)), ((), ())), preferred_element_type=F32)


def dot(a, b):
    return jnp.dot(a, b, preferred_element_type=F32)


def level(u, first, second, third, flip, mid, n):
    groups = first.shape[0]
    width = PAIR * 4 * SUB
    for g in range(groups):
        slot = flip.at[g % 2]
        lhs = first[g][:, : 5 * SUB].astype(BF)
        for j in range(0, n, 2):
            a = dot(lhs, jnp.concatenate([u(j), u(j + 1)], axis=1))
            for h in range(2):
                for t in range(PAIR * 4):
                    slot[pl.ds(t * SUB + j + h, n, stride=width), :] = a[
                        t * TROW : t * TROW + n, h * LANES : (h + 1) * LANES
                    ]
        lhs = second[g].astype(BF)
        for l in range(0, n, 2):
            rhs = jnp.concatenate(
                [slot[l * width : (l + 1) * width, :], slot[(l + 1) * width : (l + 2) * width, :]],
                axis=1,
            ).astype(BF)
            b = dot(lhs, rhs).astype(BF)
            for h in range(2):
                for q in range(PAIR * 2):
                    at = (g * PAIR * 2 + q) * LANES
                    mid[(l + h) * SUB : (l + h + 1) * SUB, at : at + LANES] = b[
                        q * SUB : (q + 1) * SUB, h * LANES : (h + 1) * LANES
                    ]
    return dot_t(mid[...], third[...])


def single(u, first, second, third, slot, mid, n):
    for j in range(0, n, 2):
        a = dot(first, jnp.concatenate([u(j), u(j + 1)], axis=1))
        for h in range(2):
            slot[pl.ds(j + h, n, stride=SUB), :] = a[:n, h * LANES : (h + 1) * LANES]
    for l in range(0, n, 2):
        rhs = jnp.concatenate(
            [slot[l * SUB : l * SUB + n, :], slot[(l + 1) * SUB : (l + 1) * SUB + n, :]], axis=1
        ).astype(BF)
        b = dot(second[:, :n], rhs).astype(BF)
        for h in range(2):
            mid[(l + h) * SUB : (l + h + 1) * SUB, :LANES] = b[:, h * LANES : (h + 1) * LANES]
    return dot_t(mid[:, :LANES], third)


def filter_kernel(px, py, u_ref, filters, out, flip, mid, spare, boxes):
    n = u_ref.shape[0]
    spare[...] = jnp.zeros_like(spare)
    fx, fy = small(filters[px[0]], spare, 0), small(filters[py[0]], spare, 1)
    spare[...] = jnp.zeros_like(spare)
    fz = pair_mats(filters, spare, boxes, boxes // 2, n)
    s = single(lambda j: u_ref[j], fx, fy, fz, flip.at[0], mid, n)
    out[...] = s.reshape(n, SUB, LANES).astype(out.dtype)


def fine_kernel(u_ref, blk, out, flip, mid, pad, first, second, third, boxes):
    n = u_ref.shape[0]
    flip[...] = jnp.zeros_like(flip)
    level_mats(blk, pad, first, second, third, boxes)
    out[...] = level(lambda j: u_ref[j], first, second, third, flip, mid, n).reshape(out.shape)


def coarse_kernel(
    px, py, u_ref, blk, turned, fine, out, flip, mid, pad, first, second, third, res, spare, boxes
):
    n = u_ref.shape[0]
    flip[...] = jnp.zeros_like(flip)
    level_mats(blk, pad, first, second, third, boxes // 2)
    s = level(lambda j: u_ref[j], first, second, third, flip, mid, n)
    res[...] = s.reshape(n, SUB, LANES).astype(BF)
    spare[...] = jnp.zeros_like(spare)
    ex, ey = small(turned[px[0]], spare, 0), small(turned[py[0]], spare, 1)
    spare[...] = jnp.zeros_like(spare)
    ez = pair_mats(turned, spare, boxes // 2, boxes, n)
    s = single(lambda j: res[j], ex, ey, ez, flip.at[0], mid, n)
    out[...] = fine[...] + s.reshape(out.shape)


def scratch(n, terms, whole=True):
    out = [
        pltpu.VMEM((2, n * PAIR * 4 * SUB, LANES), F32),
        pltpu.VMEM((n * SUB, terms * 2 * LANES), BF),
    ]
    if whole:
        groups = terms // PAIR
        out += [
            pltpu.VMEM((3 * terms * TROW, LANES), F32),
            pltpu.VMEM((groups, PAIR * 4 * TROW, 2 * LANES), F32),
            pltpu.VMEM((groups, PAIR * 2 * SUB, 2 * LANES), F32),
            pltpu.VMEM((LANES, terms * 2 * LANES), BF),
        ]
    return out


VM = pl.BlockSpec(memory_space=pltpu.VMEM)
SM = pl.BlockSpec(memory_space=pltpu.SMEM)
SPARE = pltpu.VMEM((2 * SUB, LANES), F32)
PARAMS = pltpu.CompilerParams(vmem_limit_bytes=60 * 1024 * 1024)


def shards(fine_source, fine_blocks, coarse_blocks, filters):
    boxes = fine_source.shape[2]
    terms, n = fine_blocks.shape[1], fine_blocks.shape[2]
    raw = fine_source.reshape(boxes, n, n, n)
    own = raw.transpose(2, 1, 0, 3).reshape(n, n, boxes * n)
    own = jnp.pad(own, ((0, 0), (0, SUB - n), (0, LANES - boxes * n)))
    parity_x = lax.axis_index("gx") % 2
    parity_y = lax.axis_index("gy") % 2
    px, py = parity_x.reshape(1), parity_y.reshape(1)
    turned = filters.swapaxes(1, 2)
    grid_out = jax.ShapeDtypeStruct((n, SUB, LANES), BF)
    partial = pl.pallas_call(
        functools.partial(filter_kernel, boxes=boxes),
        out_shape=grid_out,
        in_specs=[SM, SM, VM, VM],
        out_specs=VM,
        scratch_shapes=scratch(n, terms, False) + [SPARE],
        compiler_params=PARAMS,
    )(px, py, own, filters)
    sides = [shifted(own, "gx", -1), shifted(own, "gx", 1)]
    sides += [shifted(own, "gy", -1), shifted(own, "gy", 1)]
    fine_u = jnp.concatenate([own] + sides, axis=1)
    half = partial.astype(F32) + partner(partial, "gx").astype(F32)
    parent = (half + partner(half.astype(BF), "gy").astype(F32)).astype(BF)
    near = [shifted(parent, "gy", -2), shifted(parent, "gy", 2)]
    near += [shifted(parent, "gx", -2), shifted(parent, "gx", 2)]
    coarse_u = jnp.concatenate([parent] + near, axis=1)
    fine = pl.pallas_call(
        functools.partial(fine_kernel, boxes=boxes),
        out_shape=jax.ShapeDtypeStruct((n, SUB, LANES), F32),
        scratch_shapes=scratch(n, terms),
        compiler_params=PARAMS,
        cost_estimate=pl.CostEstimate(flops=4_000_000_000, bytes_accessed=4_000_000, transcendentals=0),
    )(fine_u, fine_blocks.reshape(3 * terms, n, n))
    out = pl.pallas_call(
        functools.partial(coarse_kernel, boxes=boxes),
        in_specs=[SM, SM, VM, VM, VM, VM],
        out_specs=VM,
        out_shape=jax.ShapeDtypeStruct((n, SUB, LANES), F32),
        scratch_shapes=scratch(n, terms) + [pltpu.VMEM((n, SUB, LANES), BF), SPARE],
        compiler_params=PARAMS,
    )(px, py, coarse_u, coarse_blocks.reshape(3 * terms, n, n), turned, fine)
    out = out[:, :n, : boxes * n].reshape(n, n, boxes, n).transpose(2, 0, 1, 3)
    return out.reshape(1, 1, boxes, n * n * n)


def solution(mesh):
    in_specs = (P("gx", "gy", None, None), P(), P(), P())
    out_specs = P("gx", "gy", None, None)
    return jax.shard_map(shards, mesh=mesh, in_specs=in_specs, out_specs=out_specs, check_vma=False)
```

profile of v0, /device:TPU:0, one launch (start us, length us, event | category | flops | bytes accessed | tf_op | source)
XLA Modules:
  0.0 70.0 jit_solution(13487544349053474121)
XLA Ops:
  0.0 0.0 copy-start.3
  0.0 1.3 %copy.10.filters = bf16[2,20,20]{2,1,0:T(8,128)(2,1)} copy(bf16[2,20,20]{2,0,1:T(2,128)(2,1)} %param.7) | data formatting | bytes 3200 | tf_op args[3]
  1.3 0.0 copy-done.3
  1.3 0.5 reshape.26
  1.8 0.2 copy.9
  2.0 0.2 reshape.27
  2.3 0.7 %constant_dynamic-update-slice_fusion.9 = (bf16[20,160,128]{2,1,0:T(8,128)(2,1)S(1)}, bf16[20,32,128]{2,1,0:T(8,128)(2,1)}) fusion(bf16[20,20,80]{2,1,0:T(8,128)(2,1)S(1)} %reshape.27), kind=kLoop, calls=%fused_computation.13 | loop fusion | bytes 391680
  3.0 0.0 copy-start.2
  3.0 0.0 copy-start.4
  3.0 2.4 %shard_map.46 = bf16[20,32,128]{2,1,0:T(8,128)(2,1)} custom-call(s32[1]{0:T(128)} %bitcast.px, s32[1]{0:T(128)} %bitcast.1.py, bf16[20,32,128]{2,1,0:T(8,128)(2,1)} %get-tuple-element.8.u_ref, bf16[2,20,20]{2,1,0:T(8,128)(2,1)} %copy.10.filters), custom_call_target="tpu_custom_call" | custom-call | tf_op jit(solution)/shard_map/pallas_call | solution.py:220
  5.4 0.5 collective-permute-start
  5.9 0.0 copy-done.2
  5.9 4.4 %collective-permute-start.9 = (bf16[20,32,128]{2,1,0:T(8,128)(2,1)S(1)}, bf16[20,32,128]{2,1,0:T(8,128)(2,1)S(1)}, u32[]{:S(2)}, u32[]{:S(2)}) collective-permute-start(bf16[20,32,128]{2,1,0:T(8,128)(2,1)S(1)} %copy-done.2), channel_id=1, source_target_pairs={{0,1},{1,2},{2,3},{3,4},{4,5},{5,6},{6,7},{8,9},{9,10},{10,11},{11... | collective-permute-start | bytes 491528 | tf_op jit(solution)/shard_map/ppermute | solution.py:20
  10.3 1.3 %collective-permute-start.8 = (bf16[20,32,128]{2,1,0:T(8,128)(2,1)S(1)}, bf16[20,32,128]{2,1,0:T(8,128)(2,1)S(1)}, u32[]{:S(2)}, u32[]{:S(2)}) collective-permute-start(bf16[20,32,128]{2,1,0:T(8,128)(2,1)S(1)} %copy-done.2), channel_id=1, source_target_pairs={{1,0},{2,1},{3,2},{4,3},{5,4},{6,5},{7,6},{9,8},{10,9},{11,10},{12... | collective-permute-start | bytes 491528 | tf_op jit(solution)/shard_map/ppermute | solution.py:20
  11.6 2.1 %collective-permute-start.7 = (bf16[20,32,128]{2,1,0:T(8,128)(2,1)S(1)}, bf16[20,32,128]{2,1,0:T(8,128)(2,1)S(1)}, u32[]{:S(2)}, u32[]{:S(2)}) collective-permute-start(bf16[20,32,128]{2,1,0:T(8,128)(2,1)S(1)} %copy-done.2), channel_id=1, source_target_pairs={{0,8},{8,16},{16,24},{1,9},{9,17},{17,25},{2,10},{10,18},{18,26},{... | collective-permute-start | bytes 491528 | tf_op jit(solution)/shard_map/ppermute | solution.py:20
  13.7 1.3 %collective-permute-start.6 = (bf16[20,32,128]{2,1,0:T(8,128)(2,1)S(1)}, bf16[20,32,128]{2,1,0:T(8,128)(2,1)S(1)}, u32[]{:S(2)}, u32[]{:S(2)}) collective-permute-start(bf16[20,32,128]{2,1,0:T(8,128)(2,1)S(1)} %copy-done.2), channel_id=1, source_target_pairs={{8,0},{16,8},{24,16},{9,1},{17,9},{25,17},{10,2},{18,10},{26,18},{... | collective-permute-start | bytes 491528 | tf_op jit(solution)/shard_map/ppermute | solution.py:20
  15.0 0.0 copy-done.4
  15.0 0.7 %copy.11 = bf16[2,20,20]{1,2,0:T(8,128)(2,1)} copy(bf16[2,20,20]{2,0,1:T(2,128)(2,1)S(1)} %copy-done.4) | data formatting | bytes 3200 | tf_op args[3]
  15.8 0.0 collective-permute-done
  15.8 1.0 %fusion = bf16[20,32,128]{2,1,0:T(8,128)(2,1)S(1)} fusion(bf16[20,32,128]{2,1,0:T(8,128)(2,1)S(1)} %collective-permute-done, bf16[20,32,128]{2,1,0:T(8,128)(2,1)} %shard_map.46), kind=kLoop, calls=%fused_computation.3 | loop fusion | flops 327680 | bytes 491520 | tf_op jit(solution)/shard_map/convert_element_type | solution.py:232
  16.7 2.4 %collective-permute-start.1 = (bf16[20,32,128]{2,1,0:T(8,128)(2,1)S(1)}, bf16[20,32,128]{2,1,0:T(8,128)(2,1)S(1)}, u32[]{:S(2)}, u32[]{:S(2)}) collective-permute-start(bf16[20,32,128]{2,1,0:T(8,128)(2,1)S(1)} %fusion), channel_id=1, source_target_pairs={{0,1},{1,0},{2,3},{3,2},{4,5},{5,4},{6,7},{7,6},{8,9},{9,8},{10,11... | collective-permute-start | bytes 491528 | tf_op jit(solution)/shard_map/ppermute | solution.py:25
  19.2 0.0 collective-permute-done.6
  19.2 0.0 collective-permute-done.7
  19.2 0.0 collective-permute-done.8
  19.3 0.0 copy-start
  19.3 0.0 collective-permute-done.9
  19.3 0.0 copy-start.5
  19.3 3.3 %collective-permute-done.1 = bf16[20,32,128]{2,1,0:T(8,128)(2,1)S(1)} collective-permute-done((bf16[20,32,128]{2,1,0:T(8,128)(2,1)S(1)}, bf16[20,32,128]{2,1,0:T(8,128)(2,1)S(1)}, u32[]{:S(2)}, u32[]{:S(2)}) %collective-permute-start.1) | collective-permute-done | bytes 163872 | tf_op jit(solution)/shard_map/ppermute | solution.py:25
  22.6 0.0 copy-done
  22.6 0.1 constant_dynamic-update-slice_fusion.4
  22.7 5.2 %collective-permute-start.3 = (bf16[20,32,128]{2,1,0:T(8,128)(2,1)S(1)}, bf16[20,32,128]{2,1,0:T(8,128)(2,1)S(1)}, u32[]{:S(2)}, u32[]{:S(2)}) collective-permute-start(bf16[20,32,128]{2,1,0:T(8,128)(2,1)S(1)} %get-tuple-element.6), channel_id=1, source_target_pairs={{0,2},{1,3},{2,4},{3,5},{4,6},{5,7},{8,10},{9,11},{10,12},{11,13},... | collective-permute-start | bytes 491528 | tf_op jit(solution)/shard_map/ppermute | solution.py:20
  27.9 1.3 %collective-permute-start.2 = (bf16[20,32,128]{2,1,0:T(8,128)(2,1)S(1)}, bf16[20,32,128]{2,1,0:T(8,128)(2,1)S(1)}, u32[]{:S(2)}, u32[]{:S(2)}) collective-permute-start(bf16[20,32,128]{2,1,0:T(8,128)(2,1)S(1)} %get-tuple-element.6), channel_id=1, source_target_pairs={{2,0},{3,1},{4,2},{5,3},{6,4},{7,5},{10,8},{11,9},{12,10},{13,11},... | collective-permute-start | bytes 491528 | tf_op jit(solution)/shard_map/ppermute | solution.py:20
  29.2 0.0 copy-done.5
  29.2 11.9 %shard_map.47.fine = f32[20,32,128]{2,1,0:T(8,128)} custom-call(bf16[20,160,128]{2,1,0:T(8,128)(2,1)} %copy-done.5, bf16[36,20,20]{2,1,0:T(8,128)(2,1)} %bitcast.13), custom_call_target="tpu_custom_call" | custom-call | flops 4000000000 | bytes 4000000 | tf_op jit(solution)/shard_map/pallas_call | solution.py:236
  41.1 5.4 %collective-permute-start.5 = (bf16[20,32,128]{2,1,0:T(8,128)(2,1)S(1)}, bf16[20,32,128]{2,1,0:T(8,128)(2,1)S(1)}, u32[]{:S(2)}, u32[]{:S(2)}) collective-permute-start(bf16[20,32,128]{2,1,0:T(8,128)(2,1)S(1)} %get-tuple-element.6), channel_id=1, source_target_pairs={{0,16},{8,24},{1,17},{9,25},{2,18},{10,26},{3,19},{11,27},{4,20},{... | collective-permute-start | bytes 491528 | tf_op jit(solution)/shard_map/ppermute | solution.py:20
  46.5 1.5 %collective-permute-start.4 = (bf16[20,32,128]{2,1,0:T(8,128)(2,1)S(1)}, bf16[20,32,128]{2,1,0:T(8,128)(2,1)S(1)}, u32[]{:S(2)}, u32[]{:S(2)}) collective-permute-start(bf16[20,32,128]{2,1,0:T(8,128)(2,1)S(1)} %get-tuple-element.6), channel_id=1, source_target_pairs={{16,0},{24,8},{17,1},{25,9},{18,2},{26,10},{19,3},{27,11},{20,4},{... | collective-permute-start | bytes 491528 | tf_op jit(solution)/shard_map/ppermute | solution.py:20
  48.0 0.0 collective-permute-done.2
  48.0 0.0 collective-permute-done.3
  48.1 5.6 %collective-permute-done.4 = bf16[20,32,128]{2,1,0:T(8,128)(2,1)S(1)} collective-permute-done((bf16[20,32,128]{2,1,0:T(8,128)(2,1)S(1)}, bf16[20,32,128]{2,1,0:T(8,128)(2,1)S(1)}, u32[]{:S(2)}, u32[]{:S(2)}) %collective-permute-start.4) | collective-permute-done | bytes 163872 | tf_op jit(solution)/shard_map/ppermute | solution.py:20
  53.7 0.0 collective-permute-done.5
  53.8 0.0 copy-start.1
  53.8 0.9 %copy-done.1 = bf16[20,160,128]{2,1,0:T(8,128)(2,1)} copy-done((bf16[20,160,128]{2,1,0:T(8,128)(2,1)}, bf16[20,160,128]{2,1,0:T(8,128)(2,1)S(1)}, u32[]{:S(2)}) %copy-start.1) | copy-done | bytes 819224
  54.7 12.8 %shard_map.48 = f32[20,32,128]{2,1,0:T(8,128)} custom-call(s32[1]{0:T(128)} %bitcast.px, s32[1]{0:T(128)} %bitcast.1.py, bf16[20,160,128]{2,1,0:T(8,128)(2,1)} %copy-done.1, bf16[36,20,20]{2,1,0:T(8,128)(2,1)} %bitcast.11, bf16[2,20,20]{2,1,0:T(8,128)(2,1)} %bitcast.12, f32[20,32,128]{2,1,0:T(8,128)} %shard_map.47.fine), custom_call_target="tpu_custom_call" | custom-call | tf_op jit(solution)/shard_map/pallas_call | solution.py:243
  67.5 1.0 %slice.4 = f32[20,20,80]{2,1,0:T(8,128)S(1)} slice(f32[20,32,128]{2,1,0:T(8,128)} %shard_map.48), slice={[0:20], [0:20], [0:80]} | slice | bytes 256000 | tf_op jit(solution)/shard_map/slice | solution.py:251
  68.5 0.4 reshape.30
  68.8 0.1 copy.14
  68.9 1.1 %reshape.31 = f32[1,1,4,8000]{3,2,1,0:T(4,128)} reshape(f32[4,20,20,20]{3,2,1,0:T(8,128)S(1)} %bitcast.9) | data formatting | bytes 256000 | tf_op jit(solution)/shard_map/reshape | solution.py:252
  (8 shorter events, 0.2 us)
Async XLA Ops:
  0.0 1.3 %copy-start.3 = (bf16[1,1,4,8000]{3,2,1,0:T(4,128)(2,1)S(1)}, bf16[1,1,4,8000]{3,2,1,0:T(4,128)(2,1)}, u32[]{:S(2)}) copy-start(bf16[1,1,4,8000]{3,2,1,0:T(4,128)(2,1)} %param.4) | copy-start | bytes 192004
  3.0 2.9 %copy-start.2 = (bf16[20,32,128]{2,1,0:T(8,128)(2,1)S(1)}, bf16[20,32,128]{2,1,0:T(8,128)(2,1)}, u32[]{:S(2)}) copy-start(bf16[20,32,128]{2,1,0:T(8,128)(2,1)} %get-tuple-element.8.u_ref) | copy-start | bytes 491524
  3.0 12.1 %copy-start.4 = (bf16[2,20,20]{2,0,1:T(2,128)(2,1)S(1)}, bf16[2,20,20]{2,0,1:T(2,128)(2,1)}, u32[]{:S(2)}) copy-start(bf16[2,20,20]{2,0,1:T(2,128)(2,1)} %param.7) | copy-start | bytes 4804
  5.4 10.4 %collective-permute-start = (bf16[20,32,128]{2,1,0:T(8,128)(2,1)}, bf16[20,32,128]{2,1,0:T(8,128)(2,1)S(1)}, u32[]{:S(2)}, u32[]{:S(2)}) collective-permute-start(bf16[20,32,128]{2,1,0:T(8,128)(2,1)} %shard_map.46), channel_id=1, source_target_pairs={{0,8},{8,0},{16,24},{24,16},{1,9},{9,1},{17,25},{25,17},{2,10},{10... | collective-permute-start | bytes 491528 | tf_op jit(solution)/shard_map/ppermute | solution.py:25
  5.9 13.4 %collective-permute-start.9 = (bf16[20,32,128]{2,1,0:T(8,128)(2,1)S(1)}, bf16[20,32,128]{2,1,0:T(8,128)(2,1)S(1)}, u32[]{:S(2)}, u32[]{:S(2)}) collective-permute-start(bf16[20,32,128]{2,1,0:T(8,128)(2,1)S(1)} %copy-done.2), channel_id=1, source_target_pairs={{0,1},{1,2},{2,3},{3,4},{4,5},{5,6},{6,7},{8,9},{9,10},{10,11},{11... | collective-permute-start | bytes 491528 | tf_op jit(solution)/shard_map/ppermute | solution.py:20
  10.3 8.9 %collective-permute-start.8 = (bf16[20,32,128]{2,1,0:T(8,128)(2,1)S(1)}, bf16[20,32,128]{2,1,0:T(8,128)(2,1)S(1)}, u32[]{:S(2)}, u32[]{:S(2)}) collective-permute-start(bf16[20,32,128]{2,1,0:T(8,128)(2,1)S(1)} %copy-done.2), channel_id=1, source_target_pairs={{1,0},{2,1},{3,2},{4,3},{5,4},{6,5},{7,6},{9,8},{10,9},{11,10},{12... | collective-permute-start | bytes 491528 | tf_op jit(solution)/shard_map/ppermute | solution.py:20
  11.6 7.6 %collective-permute-start.7 = (bf16[20,32,128]{2,1,0:T(8,128)(2,1)S(1)}, bf16[20,32,128]{2,1,0:T(8,128)(2,1)S(1)}, u32[]{:S(2)}, u32[]{:S(2)}) collective-permute-start(bf16[20,32,128]{2,1,0:T(8,128)(2,1)S(1)} %copy-done.2), channel_id=1, source_target_pairs={{0,8},{8,16},{16,24},{1,9},{9,17},{17,25},{2,10},{10,18},{18,26},{... | collective-permute-start | bytes 491528 | tf_op jit(solution)/shard_map/ppermute | solution.py:20
  13.7 5.4 %collective-permute-start.6 = (bf16[20,32,128]{2,1,0:T(8,128)(2,1)S(1)}, bf16[20,32,128]{2,1,0:T(8,128)(2,1)S(1)}, u32[]{:S(2)}, u32[]{:S(2)}) collective-permute-start(bf16[20,32,128]{2,1,0:T(8,128)(2,1)S(1)} %copy-done.2), channel_id=1, source_target_pairs={{8,0},{16,8},{24,16},{9,1},{17,9},{25,17},{10,2},{18,10},{26,18},{... | collective-permute-start | bytes 491528 | tf_op jit(solution)/shard_map/ppermute | solution.py:20
  16.7 5.9 %collective-permute-start.1 = (bf16[20,32,128]{2,1,0:T(8,128)(2,1)S(1)}, bf16[20,32,128]{2,1,0:T(8,128)(2,1)S(1)}, u32[]{:S(2)}, u32[]{:S(2)}) collective-permute-start(bf16[20,32,128]{2,1,0:T(8,128)(2,1)S(1)} %fusion), channel_id=1, source_target_pairs={{0,1},{1,0},{2,3},{3,2},{4,5},{5,4},{6,7},{7,6},{8,9},{9,8},{10,11... | collective-permute-start | bytes 491528 | tf_op jit(solution)/shard_map/ppermute | solution.py:25
  19.3 3.3 %copy-start = (bf16[20,32,128]{2,1,0:T(8,128)(2,1)S(1)}, bf16[20,32,128]{2,1,0:T(8,128)(2,1)}, u32[]{:S(2)}) copy-start(bf16[20,32,128]{2,1,0:T(8,128)(2,1)} %shard_map.46) | copy-start | bytes 491524
  19.3 9.8 %copy-start.5 = (bf16[20,160,128]{2,1,0:T(8,128)(2,1)}, bf16[20,160,128]{2,1,0:T(8,128)(2,1)S(1)}, u32[]{:S(2)}) copy-start(bf16[20,160,128]{2,1,0:T(8,128)(2,1)S(1)} %constant_dynamic-update-slice_fusion.5.u_ref) | copy-start | bytes 2457604
  22.7 25.3 %collective-permute-start.3 = (bf16[20,32,128]{2,1,0:T(8,128)(2,1)S(1)}, bf16[20,32,128]{2,1,0:T(8,128)(2,1)S(1)}, u32[]{:S(2)}, u32[]{:S(2)}) collective-permute-start(bf16[20,32,128]{2,1,0:T(8,128)(2,1)S(1)} %get-tuple-element.6), channel_id=1, source_target_pairs={{0,2},{1,3},{2,4},{3,5},{4,6},{5,7},{8,10},{9,11},{10,12},{11,13},... | collective-permute-start | bytes 491528 | tf_op jit(solution)/shard_map/ppermute | solution.py:20
  27.9 20.1 %collective-permute-start.2 = (bf16[20,32,128]{2,1,0:T(8,128)(2,1)S(1)}, bf16[20,32,128]{2,1,0:T(8,128)(2,1)S(1)}, u32[]{:S(2)}, u32[]{:S(2)}) collective-permute-start(bf16[20,32,128]{2,1,0:T(8,128)(2,1)S(1)} %get-tuple-element.6), channel_id=1, source_target_pairs={{2,0},{3,1},{4,2},{5,3},{6,4},{7,5},{10,8},{11,9},{12,10},{13,11},... | collective-permute-start | bytes 491528 | tf_op jit(solution)/shard_map/ppermute | solution.py:20
  41.1 12.6 %collective-permute-start.5 = (bf16[20,32,128]{2,1,0:T(8,128)(2,1)S(1)}, bf16[20,32,128]{2,1,0:T(8,128)(2,1)S(1)}, u32[]{:S(2)}, u32[]{:S(2)}) collective-permute-start(bf16[20,32,128]{2,1,0:T(8,128)(2,1)S(1)} %get-tuple-element.6), channel_id=1, source_target_pairs={{0,16},{8,24},{1,17},{9,25},{2,18},{10,26},{3,19},{11,27},{4,20},{... | collective-permute-start | bytes 491528 | tf_op jit(solution)/shard_map/ppermute | solution.py:20
  46.5 7.2 %collective-permute-start.4 = (bf16[20,32,128]{2,1,0:T(8,128)(2,1)S(1)}, bf16[20,32,128]{2,1,0:T(8,128)(2,1)S(1)}, u32[]{:S(2)}, u32[]{:S(2)}) collective-permute-start(bf16[20,32,128]{2,1,0:T(8,128)(2,1)S(1)} %get-tuple-element.6), channel_id=1, source_target_pairs={{16,0},{24,8},{17,1},{25,9},{18,2},{26,10},{19,3},{27,11},{20,4},{... | collective-permute-start | bytes 491528 | tf_op jit(solution)/shard_map/ppermute | solution.py:20
  53.8 0.9 %copy-start.1 = (bf16[20,160,128]{2,1,0:T(8,128)(2,1)}, bf16[20,160,128]{2,1,0:T(8,128)(2,1)S(1)}, u32[]{:S(2)}) copy-start(bf16[20,160,128]{2,1,0:T(8,128)(2,1)S(1)} %constant_dynamic-update-slice_fusion.u_ref) | copy-start | bytes 2457604
where the time goes:
time: 70.5 us; the launch traced here: 70 us
  Pallas kernels  27.2 us (39%)
  starting transfers between devices  25.4 us (36%)
  waiting for transfers between devices  8.95 us (13%)
  local copies, waits for them, and re-layouts  7.28 us (10%)
  other arithmetic  1.03 us (1%)
    ppermute x8, starting transfers between devices, shifted(): return lax.ppermute(block, axis, route)  22.4 us
    pallas_call x1, Pallas kernels, shards(): pl.pallas_call(functools.partial(coarse_kernel, boxes=boxes), in_specs=[S...  12.8 us
    pallas_call x1, Pallas kernels, shards(): pl.pallas_call(functools.partial(fine_kernel, boxes=boxes), out_shape=jax...  11.9 us
    ppermute x8, waiting for transfers between devices, shifted(): return lax.ppermute(block, axis, route)  5.67 us
    unnamed x21, local copies, waits for them, and re-layouts  3.78 us
    ppermute x2, waiting for transfers between devices, partner(): return lax.ppermute(block, axis, [(i, i ^ 1) for i in range(count)])  3.28 us
    ppermute x2, starting transfers between devices, partner(): return lax.ppermute(block, axis, [(i, i ^ 1) for i in range(count)])  2.92 us
    pallas_call x1, Pallas kernels, shards(): pl.pallas_call(functools.partial(filter_kernel, boxes=boxes), out_shape=g...  2.39 us
  transfers between devices with their start and end apart: 10, of which 2 were waited for; matrix products, arithmetic and copies ran while one was open for 3% of the time, Pallas kernels for 17%

commit v1 on v0

v1 whole, which is shorter than its diff:
```python
import functools

import jax
import jax.numpy as jnp
from jax import lax
from jax.experimental import pallas as pl
from jax.experimental.pallas import tpu as pltpu
from jax.sharding import PartitionSpec as P

BF = jnp.bfloat16
F32 = jnp.float32
MESH = pl.DeviceIdType.MESH
ROW = 24
PAD = 32
LANES = 128
COLS = 5


def dot(a, b):
    return jnp.dot(a, b, preferred_element_type=F32)


def dot_t(a, b):
    return lax.dot_general(a, b, (((1,), (1,)), ((), ())), preferred_element_type=F32)


def grid2(rows, cols):
    r = lax.broadcasted_iota(jnp.int32, (rows, cols), 0)
    c = lax.broadcasted_iota(jnp.int32, (rows, cols), 1)
    return r, c


def one(cond):
    return jnp.where(cond, 1.0, 0.0).astype(BF)


def repeat_lanes(rows, period, valid):
    r, c = grid2(rows, LANES)
    return one((lax.rem(c, period) == r) & (c < valid))


def repeat_rows(cols, period, valid):
    r, c = grid2(LANES, cols)
    return one((lax.rem(r, period) == c) & (r < valid))


def pad_blocks(blk, pad, n):
    pad[...] = jnp.zeros_like(pad)
    for p in range(blk.shape[0]):
        pad[p * ROW : p * ROW + n, :n] = blk[p].astype(F32)


def three(pad, m, terms):
    return [pad[(e * terms + m) * ROW : (e * terms + m + 1) * ROW, :] for e in range(3)]


def build_first(pad, first, terms, grow):
    for m in range(terms):
        low, mid, up = three(pad, m, terms)
        rows = jnp.concatenate(
            [
                mid + pltpu.roll(up, ROW, 1) + pltpu.roll(low, 2 * ROW, 1),
                pltpu.roll(mid, 3 * ROW, 1),
                pltpu.roll(mid, 4 * ROW, 1),
                mid,
            ],
            axis=0,
        ).astype(BF)
        if grow is not None:
            rows = dot(grow, rows).astype(BF)
        first[m * 4 * ROW : (m + 1) * 4 * ROW, :] = rows


def widen(source, spread, wide, out, n, count, lanes):
    wide[: source.shape[0], :lanes] = dot(source, spread)
    r, c = grid2(16, lanes)
    keep = lax.rem(c, 8) == lax.rem(r, 8)

    def body(m, carry):
        base = pl.multiple_of(m * ROW, 8)
        block = wide[pl.ds(base, ROW), :lanes]
        for i in range(0, n, 2):
            pair = jnp.concatenate(
                [jnp.broadcast_to(block[i + h : i + h + 1, :], (8, lanes)) for h in range(2)], axis=0
            )
            out[m, i * 8 : (i + 2) * 8, :lanes] = jnp.where(keep, pair, 0.0).astype(BF)
        return carry

    if count == 1:
        body(0, 0)
    else:
        lax.fori_loop(0, count, body, 0)


def spread_eight(n, lanes, groups):
    r, c = grid2(LANES, lanes)
    n8 = n * 8
    return one((r == lax.div(c, n8) * PAD + lax.div(lax.rem(c, n8), 8)) & (c < groups * n8))


def build_second(pad, second, wide, terms, n, grow):
    cats = []
    for m in range(terms):
        low, mid, up = three(pad, m, terms)
        cats.append((mid + pltpu.roll(up, PAD, 1) + pltpu.roll(low, 2 * PAD, 1)).astype(BF))
    if grow is not None:
        cats = [
            dot(grow, jnp.concatenate(cats[m : m + 4], axis=0)).astype(BF) for m in range(0, terms, 4)
        ]
    source = jnp.concatenate(cats, axis=0)
    widen(source, spread_eight(n, 4 * LANES, 3), wide, second, n, terms, 4 * LANES)


def build_third(pad, third, terms, boxes, n, grow):
    valid = boxes * n
    wide = dot(pad[:, :PAD].astype(BF), repeat_lanes(PAD, n, valid)).astype(BF)
    left = repeat_rows(ROW, n, valid)
    r, c = grid2(LANES, LANES)
    row, col = lax.div(r, n), lax.div(c, n)
    for m in range(terms):
        low, mid, up = (
            dot(left, wide[(e * terms + m) * ROW : (e * terms + m + 1) * ROW]) for e in range(3)
        )
        at = m * 2 * LANES
        tile = jnp.concatenate(
            [
                jnp.where(row == col, mid, 0.0),
                jnp.where(col == row + 1, up, 0.0) + jnp.where(col == row - 1, low, 0.0),
            ],
            axis=1,
        ).astype(BF)
        if grow is not None:
            tile = dot(grow, tile).astype(BF)
        third[:, at : at + 2 * LANES] = tile


def pair_mats(mats, boxes_in, boxes_out, n):
    r, c = grid2(LANES, LANES)
    row, col = lax.div(r, n), lax.div(c, n)
    fine, parent = (col, row) if boxes_in > boxes_out else (row, col)
    keep = (lax.div(fine, 2) == parent) & (r < boxes_out * n) & (c < boxes_in * n)
    left = repeat_rows(PAD, n, boxes_out * n)
    right = repeat_lanes(PAD, n, boxes_in * n)
    tiles = [dot(left, dot(mats[e], right).astype(BF)) for e in range(2)]
    return jnp.where(keep, jnp.where(lax.rem(fine, 2) == 0, tiles[0], tiles[1]), 0.0).astype(BF)


def first_pass(u5, first, a, n, terms):
    def body(p, carry):
        rhs = jnp.concatenate([u5[2 * p], u5[2 * p + 1]], axis=1)
        o = dot(first[...], rhs)
        at = pl.multiple_of(p * 16, 16)
        for t in range(terms * 12):
            a[t, pl.ds(at, 16), :] = jnp.concatenate(
                [o[t * 8 : t * 8 + 8, :LANES], o[t * 8 : t * 8 + 8, LANES:]], axis=0
            ).astype(BF)
        return carry

    lax.fori_loop(0, n // 2, body, 0, unroll=5 if n % 10 == 0 else 1)


def second_pass(a, second, mid, n, terms):
    n8 = n * 8

    def body(m, carry):
        def field(f):
            return jnp.concatenate([a[(m * 4 + f) * 3 + g] for g in range(3)], axis=1)

        w = second[m]
        p = dot(w[:, : 3 * n8], jnp.concatenate([field(0), field(1), field(2)], axis=0)).astype(BF)
        q = dot(w[:, :n8], field(3)).astype(BF)
        for g in range(3):
            mid[m, g * n8 : (g + 1) * n8, :LANES] = p[:, g * LANES : (g + 1) * LANES]
            mid[m, g * n8 : (g + 1) * n8, LANES:] = q[:, g * LANES : (g + 1) * LANES]
        return carry

    lax.fori_loop(0, terms, body, 0, unroll=4 if terms % 4 == 0 else 1)


def third_pass(mid, third, terms):
    return dot_t(jnp.concatenate([mid[m] for m in range(terms)], axis=1), third[...])


def kernel(
    own,
    fine_blk,
    coarse_blk,
    filt,
    out,
    u5,
    c5,
    part,
    got,
    fpad,
    tpad,
    pad,
    wide,
    first,
    second,
    third,
    fsecond,
    fa,
    a,
    mid,
    fsend,
    frecv,
    psend,
    precv,
    csend,
    crecv,
    *,
    boxes,
    nx,
    ny,
):
    n = own.shape[0]
    n8 = n * 8
    terms = fine_blk.shape[0] // 3
    x, y = lax.axis_index("gx"), lax.axis_index("gy")
    px, py = lax.rem(x, 2), lax.rem(y, 2)
    mx, my = x + 1 - 2 * px, y + 1 - 2 * py

    near = [(x, y + 1, y < ny - 1), (x, y - 1, y > 0), (x + 1, y, x < nx - 1), (x - 1, y, x > 0)]
    far = [(x, y + 2, y < ny - 2), (x, y - 2, y > 1), (x + 2, y, x < nx - 2), (x - 2, y, x > 1)]
    mates = [(mx, y), (x, my), (mx, my)]
    back = [1, 0, 3, 2]

    def slot(c):
        return slice((c + 1) * ROW, (c + 2) * ROW)

    def near_copy(c):
        dx, dy, _ = near[c]
        b = back[c]
        return pltpu.make_async_remote_copy(
            src_ref=own,
            dst_ref=u5.at[:, slot(b), :],
            send_sem=fsend.at[c],
            recv_sem=frecv.at[b],
            device_id=(dx, dy),
            device_id_type=MESH,
        )

    def far_copy(c):
        dx, dy, _ = far[c]
        b = back[c]
        return pltpu.make_async_remote_copy(
            src_ref=c5.at[:, 0:ROW, :],
            dst_ref=c5.at[:, slot(b), :],
            send_sem=csend.at[c],
            recv_sem=crecv.at[b],
            device_id=(dx, dy),
            device_id_type=MESH,
        )

    def mate_copy(c):
        return pltpu.make_async_remote_copy(
            src_ref=part,
            dst_ref=got.at[c],
            send_sem=psend.at[c],
            recv_sem=precv.at[c],
            device_id=mates[c],
            device_id_type=MESH,
        )

    barrier = pltpu.get_barrier_semaphore()
    count = jnp.int32(1)
    pl.semaphore_signal(barrier, inc=1, device_id=mates[2], device_id_type=MESH)
    for dx, dy, exists in near + far:
        count = count + jnp.where(exists, 1, 0)

        @pl.when(exists)
        def _():
            pl.semaphore_signal(barrier, inc=1, device_id=(dx, dy), device_id_type=MESH)

    u5[:, 0:ROW, :] = own[...]
    for buf in (u5, c5):
        buf[:, COLS * ROW :, :] = jnp.zeros((n, LANES - COLS * ROW, LANES), BF)
    for group, buf in ((near, u5), (far, c5)):
        for c in range(4):

            @pl.when(jnp.logical_not(group[c][2]))
            def _():
                buf[:, slot(c), :] = jnp.zeros((n, ROW, LANES), BF)

    fpad[...] = jnp.zeros_like(fpad)
    for e in range(2):
        fpad[e, :n, :n] = filt[:, e, :].astype(F32)
    r, c = grid2(PAD, PAD)
    eye = one(r == c)
    mats = [fpad[e][:, :PAD].astype(BF) for e in range(2)]
    tpad[...] = jnp.zeros_like(tpad)
    for e in range(2):
        tpad[e, :, :PAD] = dot_t(eye, mats[e])
    turned = [tpad[e][:, :PAD].astype(BF) for e in range(2)]
    fy = fpad[py][:ROW, :ROW].astype(BF)
    fx = fpad[px][:ROW, :].astype(BF)
    widen(fx, spread_eight(n, 2 * LANES, 1), wide, fsecond, n, 1, 2 * LANES)
    fz = pair_mats(mats, boxes, boxes // 2, n)

    pl.semaphore_wait(barrier, count)
    for c in range(4):

        @pl.when(near[c][2])
        def _():
            near_copy(c).start()

    for p in range(n // 2):
        o = dot(fy, jnp.concatenate([own[2 * p], own[2 * p + 1]], axis=1))
        for g in range(3):
            fa[g, p * 16 : (p + 1) * 16, :] = jnp.concatenate(
                [o[g * 8 : g * 8 + 8, :LANES], o[g * 8 : g * 8 + 8, LANES:]], axis=0
            ).astype(BF)
    o = dot(fsecond[0][:, :n8], jnp.concatenate([fa[g] for g in range(3)], axis=1)).astype(BF)
    for g in range(3):
        s = dot_t(o[:, g * LANES : (g + 1) * LANES], fz)
        part[:, g * 8 : (g + 1) * 8, :] = s.reshape(n, 8, LANES).astype(BF)
    for c in range(3):
        mate_copy(c).start()

    pad_blocks(fine_blk, pad, n)
    build_first(pad, first, terms, None)
    build_second(pad, second, wide, terms, n, None)
    build_third(pad, third, terms, boxes, n, None)

    for c in range(3):
        mate_copy(c).wait_recv()
    total = part[...].astype(F32)
    for c in range(3):
        total = total + got[c].astype(F32)
    c5[:, 0:ROW, :] = total.astype(BF)
    for c in range(4):

        @pl.when(far[c][2])
        def _():
            far_copy(c).start()

    for c in range(4):

        @pl.when(near[c][2])
        def _():
            near_copy(back[c]).wait_recv()

    first_pass(u5, first, a, n, terms)
    second_pass(a, second, mid, n, terms)
    o = third_pass(mid, third, terms)
    for g in range(3):
        out[:, g * 8 : (g + 1) * 8, :] = o[g * n8 : (g + 1) * n8].reshape(n, 8, LANES)

    pad_blocks(coarse_blk, pad, n)
    r, c = grid2(4 * ROW, 4 * ROW)
    same = lax.div(r, ROW) == lax.div(c, ROW)
    rows4 = one(lax.rem(grid2(4 * ROW, PAD)[0], ROW) == grid2(4 * ROW, PAD)[1])
    cols4 = one(lax.rem(grid2(PAD, 4 * ROW)[1], ROW) == grid2(PAD, 4 * ROW)[0])

    def quad(mat):
        return jnp.where(same, dot(rows4, dot(mat, cols4).astype(BF)), 0.0).astype(BF)

    build_first(pad, first, terms, quad(tpad[py][:, :PAD].astype(BF)))
    build_second(pad, second, wide, terms, n, quad(tpad[px][:, :PAD].astype(BF)))
    build_third(pad, third, terms, boxes // 2, n, pair_mats(turned, boxes // 2, boxes, n))

    for c in range(4):

        @pl.when(far[c][2])
        def _():
            far_copy(back[c]).wait_recv()

    first_pass(c5, first, a, n, terms)
    second_pass(a, second, mid, n, terms)
    o = third_pass(mid, third, terms)
    for g in range(3):
        at = slice(g * 8, (g + 1) * 8)
        out[:, at, :] = out[:, at, :] + o[g * n8 : (g + 1) * n8].reshape(n, 8, LANES)

    for c in range(3):
        mate_copy(c).wait_send()
    for c in range(4):

        @pl.when(near[c][2])
        def _():
            near_copy(c).wait_send()

        @pl.when(far[c][2])
        def _():
            far_copy(c).wait_send()


VM = pl.BlockSpec(memory_space=pltpu.VMEM)


def shards(nx, ny, fine_source, fine_blocks, coarse_blocks, filters):
    boxes = fine_source.shape[2]
    terms, n = fine_blocks.shape[1], fine_blocks.shape[2]
    n8 = n * 8
    raw = fine_source.reshape(boxes, n, n, n)
    own = raw.transpose(1, 2, 0, 3).reshape(n, n, boxes * n)
    own = jnp.pad(own, ((0, 0), (0, ROW - n), (0, LANES - boxes * n)))
    dma = pltpu.SemaphoreType.DMA
    out = pl.pallas_call(
        functools.partial(kernel, boxes=boxes, nx=nx, ny=ny),
        out_shape=jax.ShapeDtypeStruct((n, ROW, LANES), F32),
        in_specs=[VM] * 4,
        out_specs=VM,
        scratch_shapes=[
            pltpu.VMEM((n, LANES, LANES), BF),
            pltpu.VMEM((n, LANES, LANES), BF),
            pltpu.VMEM((n, ROW, LANES), BF),
            pltpu.VMEM((3, n, ROW, LANES), BF),
            pltpu.VMEM((2, PAD, LANES), F32),
            pltpu.VMEM((2, PAD, LANES), F32),
            pltpu.VMEM((3 * terms * ROW, LANES), F32),
            pltpu.VMEM((terms * ROW, 4 * LANES), F32),
            pltpu.VMEM((terms * 4 * ROW, LANES), BF),
            pltpu.VMEM((terms, n8, 4 * LANES), BF),
            pltpu.VMEM((LANES, terms * 2 * LANES), BF),
            pltpu.VMEM((1, n8, 2 * LANES), BF),
            pltpu.VMEM((3, n8, LANES), BF),
            pltpu.VMEM((terms * 12, n8, LANES), BF),
            pltpu.VMEM((terms, 3 * n8, 2 * LANES), BF),
            dma((4,)),
            dma((4,)),
            dma((3,)),
            dma((3,)),
            dma((4,)),
            dma((4,)),
        ],
        compiler_params=pltpu.CompilerParams(
            vmem_limit_bytes=60 * 1024 * 1024, collective_id=0, has_side_effects=True
        ),
    )(
        own,
        fine_blocks.reshape(3 * terms, n, n),
        coarse_blocks.reshape(3 * terms, n, n),
        filters.transpose(1, 0, 2),
    )
    out = out[:, :n, : boxes * n].reshape(n, n, boxes, n).transpose(2, 0, 1, 3)
    return out.reshape(1, 1, boxes, n * n * n)


def solution(mesh):
    in_specs = (P("gx", "gy", None, None), P(), P(), P())
    out_specs = P("gx", "gy", None, None)
    body = functools.partial(shards, mesh.shape["gx"], mesh.shape["gy"])
    return jax.shard_map(body, mesh=mesh, in_specs=in_specs, out_specs=out_specs, check_vma=False)
```

time: 70.5 us -> 36.1 us (0.51)
  the two profiles are of different devices: /device:TPU:0 before, /device:TPU:9 now
where the time goes in v1:
time: 36.1 us; the launch traced here: 35.9 us
  Pallas kernels  30.9 us (86%)
  local copies, waits for them, and re-layouts  4.94 us (14%)
    pallas_call x1, Pallas kernels, shards(): pl.pallas_call(functools.partial(kernel, boxes=boxes, nx=nx, ny=ny), out_...  30.9 us
    reshape x2, local copies, waits for them, and re-layouts, shards(): out = out[:, :n, :boxes * n].reshape(n, n, boxes, n).transpose(2, 0, 1, 3)  1.39 us
    reshape x1, local copies, waits for them, and re-layouts, shards(): raw = fine_source.reshape(boxes, n, n, n)  1.3 us
    reshape x1, local copies, waits for them, and re-layouts, shards(): return out.reshape(1, 1, boxes, n * n * n)  1.11 us

profile of v1, /device:TPU:9, one launch (start us, length us, event | category | flops | bytes accessed | tf_op | source)
XLA Modules:
  0.0 35.9 jit_solution(10951144951120251998)
XLA Ops:
  0.0 1.3 %reshape.18 = bf16[4,20,20,20]{3,2,1,0:T(8,128)(2,1)S(1)} reshape(bf16[1,1,4,8000]{3,2,1,0:T(4,128)(2,1)} %param.4) | data formatting | bytes 128000 | tf_op jit(solution)/shard_map/reshape | solution.py:395
  1.3 0.2 copy.7
  1.5 0.2 reshape.19
  1.8 0.7 %pad.4.own = bf16[20,24,128]{2,1,0:T(8,128)(2,1)} pad(bf16[20,20,80]{2,1,0:T(8,128)(2,1)S(1)} %reshape.19, bf16[]{:T(256)} %constant.2.clone.1), padding=0_0x0_4x0_48 | pad | bytes 186882 | tf_op jit(solution)/shard_map/jit(_pad)/pad | solution.py:397
  2.5 30.9 %shard_map.46 = f32[20,24,128]{2,1,0:T(8,128)} custom-call(bf16[20,24,128]{2,1,0:T(8,128)(2,1)} %pad.4.own, bf16[36,20,20]{2,1,0:T(8,128)(2,1)} %bitcast.11, bf16[36,20,20]{2,1,0:T(8,128)(2,1)} %bitcast.12, bf16[20,2,20]{2,1,0:T(2,128)(2,1)} %bitcast.13), custom_call_target="tpu_custom_call" | custom-call | tf_op jit(solution)/shard_map/pallas_call | solution.py:399
  33.4 1.3 %reshape.22 = f32[20,20,4,20]{3,2,1,0:T(4,128)S(1)} reshape(f32[20,20,80]{2,1,0:T(8,128)} %bitcast.10) | data formatting | bytes 256000 | tf_op jit(solution)/shard_map/reshape | solution.py:436
  34.7 0.1 copy.10
  34.8 1.1 %reshape.23 = f32[1,1,4,8000]{3,2,1,0:T(4,128)} reshape(f32[4,20,20,20]{3,2,1,0:T(8,128)S(1)} %bitcast.8) | data formatting | bytes 256000 | tf_op jit(solution)/shard_map/reshape | solution.py:437

commit v2 on v1

v2 whole, which is shorter than its diff:
```python
import functools

import jax
import jax.numpy as jnp
from jax import lax
from jax.experimental import pallas as pl
from jax.experimental.pallas import tpu as pltpu
from jax.sharding import PartitionSpec as P

BF = jnp.bfloat16
F32 = jnp.float32
MESH = pl.DeviceIdType.MESH
ROW = 24
PAD = 32
LANES = 128


def dot(a, b):
    return jnp.dot(a, b, preferred_element_type=F32)


def dot_t(a, b):
    return lax.dot_general(a, b, (((1,), (1,)), ((), ())), preferred_element_type=F32)


def grid2(rows, cols):
    r = lax.broadcasted_iota(jnp.int32, (rows, cols), 0)
    c = lax.broadcasted_iota(jnp.int32, (rows, cols), 1)
    return r, c


def one(cond):
    return jnp.where(cond, 1.0, 0.0).astype(BF)


def repeat_lanes(rows, period, valid):
    r, c = grid2(rows, LANES)
    return one((lax.rem(c, period) == r) & (c < valid))


def repeat_rows(cols, period, valid):
    r, c = grid2(LANES, cols)
    return one((lax.rem(r, period) == c) & (r < valid))


def cats(blk, pad, n, terms):
    pad[...] = jnp.zeros_like(pad)
    for p in range(3 * terms):
        pad[p * ROW : p * ROW + n, :n] = blk[p].astype(F32)


def three(pad, m, terms):
    return [pad[(e * terms + m) * ROW : (e * terms + m + 1) * ROW, :] for e in range(3)]


def build_first(pad, first, terms):
    for m in range(terms):
        low, mid, up = three(pad, m, terms)
        first[m * ROW : (m + 1) * ROW, :] = (
            mid + pltpu.roll(up, ROW, 1) + pltpu.roll(low, 2 * ROW, 1)
        ).astype(BF)


def grown(first, mat, terms):
    step = mat.shape[0]
    rows = [dot(mat, first[m : m + step, :]).astype(BF) for m in range(0, terms * ROW, step)]
    return jnp.concatenate(rows, axis=0)


def widen(source, spread, wide, out, n, count, lanes):
    wide[: source.shape[0], :lanes] = dot(source, spread)
    r, c = grid2(16, lanes)
    keep = lax.rem(c, 8) == lax.rem(r, 8)

    def body(m, carry):
        base = pl.multiple_of(m * ROW, 8)
        block = wide[pl.ds(base, ROW), :lanes]
        for i in range(0, n, 2):
            pair = jnp.concatenate(
                [jnp.broadcast_to(block[i + h : i + h + 1, :], (8, lanes)) for h in range(2)], axis=0
            )
            out[m, i * 8 : (i + 2) * 8, :lanes] = jnp.where(keep, pair, 0.0).astype(BF)
        return carry

    if count == 1:
        body(0, 0)
    else:
        lax.fori_loop(0, count, body, 0)


def spread_eight(n, lanes, groups):
    r, c = grid2(LANES, lanes)
    n8 = n * 8
    return one((r == lax.div(c, n8) * ROW + lax.div(lax.rem(c, n8), 8)) & (c < groups * n8))


def build_second(source, second, wide, terms, n):
    widen(source, spread_eight(n, 4 * LANES, 3), wide, second, n, terms, 4 * LANES)


def build_third(pad, third, terms, boxes, n, grow):
    both = grow is not None
    wide = dot(pad[:, :PAD].astype(BF), repeat_lanes(PAD, n, boxes * n * (1 + both))).astype(BF)
    left = repeat_rows(ROW, n, boxes * n)
    r, c = grid2(LANES, LANES)
    row, col = lax.div(r, n), lax.div(c, n)
    side = col - boxes if both else col
    for m in range(terms):
        low, mid, up = (
            dot(left, wide[(e * terms + m) * ROW : (e * terms + m + 1) * ROW]) for e in range(3)
        )
        main = jnp.where((row == col) & (col < boxes), mid, 0.0)
        other = jnp.where(side == row + 1, up, 0.0)
        other = other + jnp.where((side == row - 1) & (side >= 0), low, 0.0)
        if both:
            third[:, m * LANES : (m + 1) * LANES] = dot(grow, (main + other).astype(BF)).astype(BF)
        else:
            at = m * 2 * LANES
            third[:, at : at + LANES] = main.astype(BF)
            third[:, at + LANES : at + 2 * LANES] = other.astype(BF)


def pair_mats(mats, boxes_in, boxes_out, n):
    r, c = grid2(LANES, LANES)
    row, col = lax.div(r, n), lax.div(c, n)
    fine, parent = (col, row) if boxes_in > boxes_out else (row, col)
    keep = (lax.div(fine, 2) == parent) & (r < boxes_out * n) & (c < boxes_in * n)
    left = repeat_rows(PAD, n, boxes_out * n)
    right = repeat_lanes(PAD, n, boxes_in * n)
    tiles = [dot(left, dot(mats[e], right).astype(BF)) for e in range(2)]
    return jnp.where(keep, jnp.where(lax.rem(fine, 2) == 0, tiles[0], tiles[1]), 0.0)


def lane(shape):
    return lax.broadcasted_iota(jnp.int32, shape, 1)


def pack(src, dst, n, kappa):
    at = lane((ROW, LANES))
    for q in range((n + 2) // 3):
        tile = [src[3 * q + h].astype(F32) if 3 * q + h < n else None for h in range(3)]
        r1 = pltpu.roll(tile[1], kappa, 1)
        dst[2 * q] = jnp.where(at < kappa, tile[0], r1).astype(BF)
        r2 = jnp.zeros_like(r1) if tile[2] is None else pltpu.roll(tile[2], 2 * kappa - LANES, 1)
        dst[2 * q + 1] = jnp.where(at < 2 * kappa - LANES, r1, r2).astype(BF)


def unpack(src, dst, rows, n, kappa):
    at = lane((ROW, LANES))
    for q in range((n + 2) // 3):
        a, b = src[2 * q].astype(F32), src[2 * q + 1].astype(F32)
        dst[3 * q, rows, :] = a.astype(BF)
        dst[3 * q + 1, rows, :] = pltpu.roll(jnp.where(at >= kappa, a, b), LANES - kappa, 1).astype(BF)
        if 3 * q + 2 < n:
            dst[3 * q + 2, rows, :] = pltpu.roll(b, 2 * (LANES - kappa), 1).astype(BF)


def unpack_parent(src, dst, rows, n, kappa, twice):
    at = lane((ROW, LANES))
    deep = (n + 2) // 3
    for s in range(deep):
        tile = src[s].astype(F32)
        for t in range(3):
            if t * deep + s < n:
                v = tile if t == 0 else pltpu.roll(tile, LANES - t * kappa, 1)
                other = 0.0
                if twice:
                    other = tile if t == 1 else pltpu.roll(tile, (LANES - (t - 1) * kappa) % LANES, 1)
                dst[t * deep + s, rows, :] = jnp.where(at < kappa, v, other).astype(BF)


def first_pass(u, rows, w, a, n, blocks):
    def body(p, carry):
        rhs = jnp.concatenate([u[2 * p, :rows, :], u[2 * p + 1, :rows, :]], axis=1)
        o = dot(w[:, :rows], rhs)
        at = pl.multiple_of(p * 16, 16)
        for t in range(blocks):
            a[t, pl.ds(at, 16), :] = jnp.concatenate(
                [o[t * 8 : t * 8 + 8, :LANES], o[t * 8 : t * 8 + 8, LANES:]], axis=0
            ).astype(BF)
        return carry

    lax.fori_loop(0, n // 2, body, 0, unroll=5 if n % 10 == 0 else 1)


def second_pass(fields, second, mid, n, terms, at):
    n8 = n * 8
    k = len(fields) * n8

    def body(m, carry):
        rhs = jnp.concatenate(
            [jnp.concatenate([a[m * 3 + g] for g in range(3)], axis=1) for a in fields], axis=0
        )
        p = dot(second[m][:, :k], rhs).astype(BF)
        for g in range(3):
            mid[m, g * n8 : (g + 1) * n8, at : at + LANES] = p[:, g * LANES : (g + 1) * LANES]
        return carry

    lax.fori_loop(0, terms, body, 0, unroll=4 if terms % 4 == 0 else 1)


def third_pass(mid, third, terms):
    return dot_t(jnp.concatenate([mid[m] for m in range(terms)], axis=1), third[...])


def kernel(
    own,
    fine_blk,
    coarse_blk,
    filt,
    out,
    opk,
    npk,
    u,
    ux,
    part,
    half,
    got,
    cpk,
    ppk,
    cu,
    cx,
    fpad,
    tpad,
    pad,
    wide,
    first,
    second,
    third,
    first_c,
    second_c,
    third_c,
    fsecond,
    fa,
    a,
    mid,
    mid_c,
    fsend,
    frecv,
    psend,
    precv,
    csend,
    crecv,
    *,
    boxes,
    nx,
    ny,
):
    n = own.shape[0]
    n8 = n * 8
    terms = fine_blk.shape[0] // 3
    kappa = boxes * n
    half_k = kappa // 2
    deep = (n + 2) // 3
    x, y = lax.axis_index("gx"), lax.axis_index("gy")
    px, py = lax.rem(x, 2), lax.rem(y, 2)
    mates = [(x + 1 - 2 * px, y), (x, y + 1 - 2 * py)]
    near = [(x, y + 1, y < ny - 1), (x, y - 1, y > 0), (x + 1, y, x < nx - 1), (x - 1, y, x > 0)]
    far = [(x, y + 2, y < ny - 2), (x, y - 2, y > 1), (x + 2, y, x < nx - 2), (x - 2, y, x > 1)]
    back = [1, 0, 3, 2]

    def near_copy(c):
        b = back[c]
        return pltpu.make_async_remote_copy(
            src_ref=opk.at[:, :n, :],
            dst_ref=npk.at[b, :, :n, :],
            send_sem=fsend.at[c],
            recv_sem=frecv.at[b],
            device_id=near[c][:2],
            device_id_type=MESH,
        )

    def far_copy(c):
        b = back[c]
        return pltpu.make_async_remote_copy(
            src_ref=cpk.at[:, :n, :],
            dst_ref=ppk.at[b, :, :n, :],
            send_sem=csend.at[c],
            recv_sem=crecv.at[b],
            device_id=far[c][:2],
            device_id_type=MESH,
        )

    def mate_copy(c):
        return pltpu.make_async_remote_copy(
            src_ref=(part, half)[c].at[:, :n, :],
            dst_ref=got.at[c, :, :n, :],
            send_sem=psend.at[c],
            recv_sem=precv.at[c],
            device_id=mates[c],
            device_id_type=MESH,
        )

    barrier = pltpu.get_barrier_semaphore()
    count = jnp.int32(0)
    for dx, dy, exists in near + far:
        count = count + jnp.where(exists, 1, 0)

        @pl.when(exists)
        def _():
            pl.semaphore_signal(barrier, inc=1, device_id=(dx, dy), device_id_type=MESH)

    for c in range(4):
        npk[c, :, n:, :] = jnp.zeros((2 * deep, ROW - n, LANES), BF)
        ppk[c, :, n:, :] = jnp.zeros((deep, ROW - n, LANES), BF)

        @pl.when(jnp.logical_not(near[c][2]))
        def _():
            npk[c, :, :n, :] = jnp.zeros((2 * deep, n, LANES), BF)

        @pl.when(jnp.logical_not(far[c][2]))
        def _():
            ppk[c, :, :n, :] = jnp.zeros((deep, n, LANES), BF)

    pack(own, opk, n, kappa)

    fpad[...] = jnp.zeros_like(fpad)
    for e in range(2):
        fpad[e, :n, :n] = filt[:, e, :].astype(F32)
    r, c = grid2(PAD, PAD)
    eye = one(r == c)
    mats = [fpad[e][:, :PAD].astype(BF) for e in range(2)]
    tpad[...] = jnp.zeros_like(tpad)
    for e in range(2):
        tpad[e, :, :PAD] = dot_t(eye, mats[e])
    turned = [tpad[e][:, :PAD].astype(BF) for e in range(2)]
    fy = fpad[py][:ROW, :ROW].astype(BF)
    fx = fpad[px][:ROW, :].astype(BF)
    widen(fx, spread_eight(n, 2 * LANES, 1), wide, fsecond, n, 1, 2 * LANES)
    fz = pair_mats(mats, boxes, boxes // 2, n)
    turns = [fz if t == 0 else pltpu.roll(fz, t * half_k, 0) for t in range(3)]
    fz3 = jnp.concatenate(turns, axis=1).astype(BF)

    pl.semaphore_wait(barrier, count)
    for c in (2, 3, 0, 1):

        @pl.when(near[c][2])
        def _():
            near_copy(c).start()

    for p in range(n // 2):
        o = dot(fy, jnp.concatenate([own[2 * p], own[2 * p + 1]], axis=1))
        for g in range(3):
            fa[g, p * 16 : (p + 1) * 16, :] = jnp.concatenate(
                [o[g * 8 : g * 8 + 8, :LANES], o[g * 8 : g * 8 + 8, LANES:]], axis=0
            ).astype(BF)
    o = dot(fsecond[0][:, :n8], jnp.concatenate([fa[g] for g in range(3)], axis=1))
    o = jnp.concatenate([o, jnp.zeros(((3 * deep - n) * 8, 3 * LANES), F32)], axis=0).astype(BF)
    d8 = deep * 8
    for g in range(3):
        s = dot_t(
            jnp.concatenate(
                [o[t * d8 : (t + 1) * d8, g * LANES : (g + 1) * LANES] for t in range(3)], axis=1
            ),
            fz3,
        )
        part[:, g * 8 : (g + 1) * 8, :] = s.reshape(deep, 8, LANES).astype(BF)
    mate_copy(0).start()

    cats(fine_blk, pad, n, terms)
    build_first(pad, first, terms)
    build_second(first[...], second, wide, terms, n)

    mate_copy(0).wait_recv()
    half[:, :n, :] = (part[:, :n, :].astype(F32) + got[0, :, :n, :].astype(F32)).astype(BF)
    mate_copy(1).start()

    build_third(pad, third, terms, boxes, n, None)
    first_pass(own, ROW, first, a.at[3], n, terms * 3)
    second_pass([a.at[3]], second, mid, n, terms, LANES)

    mate_copy(1).wait_recv()
    cpk[:, n:, :] = jnp.zeros((deep, ROW - n, LANES), BF)
    cpk[:, :n, :] = (half[:, :n, :].astype(F32) + got[1, :, :n, :].astype(F32)).astype(BF)
    for c in range(4):

        @pl.when(far[c][2])
        def _():
            far_copy(c).start()

    cats(coarse_blk, pad, n, terms)
    build_first(pad, first_c, terms)
    r, c = grid2(4 * ROW, 4 * ROW)
    same = lax.div(r, ROW) == lax.div(c, ROW)
    rows4 = one(lax.rem(grid2(4 * ROW, PAD)[0], ROW) == grid2(4 * ROW, PAD)[1])
    cols4 = one(lax.rem(grid2(PAD, 4 * ROW)[1], ROW) == grid2(PAD, 4 * ROW)[0])

    def quad(mat):
        return jnp.where(same, dot(rows4, dot(mat, cols4).astype(BF)), 0.0).astype(BF)

    build_second(grown(first_c, quad(tpad[px][:, :PAD].astype(BF)), terms), second_c, wide, terms, n)
    first_c[...] = grown(first_c, quad(tpad[py][:, :PAD].astype(BF)), terms)
    build_third(pad, third_c, terms, boxes // 2, n, pair_mats(turned, boxes // 2, boxes, n).astype(BF))

    def near_wait(c):
        @pl.when(near[c][2])
        def _():
            near_copy(back[c]).wait_recv()

    for c in (2, 3):
        near_wait(c)
        unpack(npk.at[c], ux.at[c - 2], slice(0, ROW), n, kappa)
        first_pass(ux.at[c - 2], ROW, first, a.at[c - 1], n, terms * 3)
    u[:, :ROW, :] = own[...]
    for c in (0, 1):
        near_wait(c)
        unpack(npk.at[c], u, slice((c + 1) * ROW, (c + 2) * ROW), n, kappa)
    first_pass(u, 3 * ROW, first, a.at[0], n, terms * 3)
    second_pass([a.at[0], a.at[1], a.at[2]], second, mid, n, terms, 0)
    o = third_pass(mid, third, terms)
    for g in range(3):
        out[:, g * 8 : (g + 1) * 8, :] = o[g * n8 : (g + 1) * n8].reshape(n, 8, LANES)

    unpack_parent(cpk, cu, slice(0, ROW), n, half_k, True)
    for c in range(4):

        @pl.when(far[c][2])
        def _():
            far_copy(back[c]).wait_recv()

        if c < 2:
            unpack_parent(ppk.at[c], cu, slice((c + 1) * ROW, (c + 2) * ROW), n, half_k, False)
        else:
            unpack_parent(ppk.at[c], cx.at[c - 2], slice(0, ROW), n, half_k, False)
    first_pass(cx.at[0], ROW, first_c, a.at[1], n, terms * 3)
    first_pass(cx.at[1], ROW, first_c, a.at[2], n, terms * 3)
    first_pass(cu, 3 * ROW, first_c, a.at[0], n, terms * 3)
    second_pass([a.at[0], a.at[1], a.at[2]], second_c, mid_c, n, terms, 0)
    o = third_pass(mid_c, third_c, terms)
    for g in range(3):
        at = slice(g * 8, (g + 1) * 8)
        out[:, at, :] = out[:, at, :] + o[g * n8 : (g + 1) * n8].reshape(n, 8, LANES)

    for c in range(2):
        mate_copy(c).wait_send()
    for c in range(4):

        @pl.when(near[c][2])
        def _():
            near_copy(c).wait_send()

        @pl.when(far[c][2])
        def _():
            far_copy(c).wait_send()


VM = pl.BlockSpec(memory_space=pltpu.VMEM)


def shards(nx, ny, fine_source, fine_blocks, coarse_blocks, filters):
    boxes = fine_source.shape[2]
    terms, n = fine_blocks.shape[1], fine_blocks.shape[2]
    n8 = n * 8
    deep = (n + 2) // 3
    raw = fine_source.reshape(boxes, n, n, n)
    own = raw.transpose(1, 2, 0, 3).reshape(n, n, boxes * n)
    own = jnp.pad(own, ((0, 0), (0, ROW - n), (0, LANES - boxes * n)))
    dma = pltpu.SemaphoreType.DMA

    def bf(*shape):
        return pltpu.VMEM(shape, BF)

    def f32(*shape):
        return pltpu.VMEM(shape, F32)

    out = pl.pallas_call(
        functools.partial(kernel, boxes=boxes, nx=nx, ny=ny),
        out_shape=jax.ShapeDtypeStruct((n, ROW, LANES), F32),
        in_specs=[VM] * 4,
        out_specs=VM,
        scratch_shapes=[
            bf(2 * deep, ROW, LANES),
            bf(4, 2 * deep, ROW, LANES),
            bf(n, 3 * ROW, LANES),
            bf(2, n, ROW, LANES),
            bf(deep, ROW, LANES),
            bf(deep, ROW, LANES),
            bf(2, deep, ROW, LANES),
            bf(deep, ROW, LANES),
            bf(4, deep, ROW, LANES),
            bf(n, 3 * ROW, LANES),
            bf(2, n, ROW, LANES),
            f32(2, PAD, LANES),
            f32(2, PAD, LANES),
            f32(3 * terms * ROW, LANES),
            f32(terms * ROW, 4 * LANES),
            bf(terms * ROW, LANES),
            bf(terms, n8, 4 * LANES),
            bf(LANES, terms * 2 * LANES),
            bf(terms * ROW, LANES),
            bf(terms, n8, 4 * LANES),
            bf(LANES, terms * LANES),
            bf(1, n8, 2 * LANES),
            bf(3, n8, LANES),
            bf(4, terms * 3, n8, LANES),
            bf(terms, 3 * n8, 2 * LANES),
            bf(terms, 3 * n8, LANES),
            dma((4,)),
            dma((4,)),
            dma((2,)),
            dma((2,)),
            dma((4,)),
            dma((4,)),
        ],
        compiler_params=pltpu.CompilerParams(
            vmem_limit_bytes=60 * 1024 * 1024, collective_id=0, has_side_effects=True
        ),
    )(
        own,
        fine_blocks.reshape(3 * terms, n, n),
        coarse_blocks.reshape(3 * terms, n, n),
        filters.transpose(1, 0, 2),
    )
    out = out[:, :n, : boxes * n].reshape(n, n, boxes, n).transpose(2, 0, 1, 3)
    return out.reshape(1, 1, boxes, n * n * n)


def solution(mesh):
    in_specs = (P("gx", "gy", None, None), P(), P(), P())
    out_specs = P("gx", "gy", None, None)
    body = functools.partial(shards, mesh.shape["gx"], mesh.shape["gy"])
    return jax.shard_map(body, mesh=mesh, in_specs=in_specs, out_specs=out_specs, check_vma=False)
```

time: 36.1 us -> 28.1 us (0.78)
  the two profiles are of different devices: /device:TPU:9 before, /device:TPU:0 now
where the time goes in v2:
time: 28.1 us; the launch traced here: 27.9 us
  Pallas kernels  22.9 us (81%)
  local copies, waits for them, and re-layouts  4.94 us (18%)
    pallas_call x1, Pallas kernels, shards(): pl.pallas_call(functools.partial(kernel, boxes=boxes, nx=nx, ny=ny), out_...  22.9 us
    reshape x2, local copies, waits for them, and re-layouts, shards(): out = out[:, :n, :boxes * n].reshape(n, n, boxes, n).transpose(2, 0, 1, 3)  1.39 us
    reshape x1, local copies, waits for them, and re-layouts, shards(): raw = fine_source.reshape(boxes, n, n, n)  1.3 us
    reshape x1, local copies, waits for them, and re-layouts, shards(): return out.reshape(1, 1, boxes, n * n * n)  1.11 us
    pad x1, local copies, waits for them, and re-layouts, shards(): own = jnp.pad(own, ((0, 0), (0, ROW - n), (0, LANES - boxes * n)))  0.68 us

profile of v2, /device:TPU:0, one launch (start us, length us, event | category | flops | bytes accessed | tf_op | source)
XLA Modules:
  0.0 27.9 jit_solution(13643145755510477656)
XLA Ops:
  0.0 1.3 %reshape.18 = bf16[4,20,20,20]{3,2,1,0:T(8,128)(2,1)S(1)} reshape(bf16[1,1,4,8000]{3,2,1,0:T(4,128)(2,1)} %param.4) | data formatting | bytes 128000 | tf_op jit(solution)/shard_map/reshape | solution.py:455
  1.3 0.2 copy.7
  1.5 0.2 reshape.19
  1.8 0.7 %pad.4.own = bf16[20,24,128]{2,1,0:T(8,128)(2,1)} pad(bf16[20,20,80]{2,1,0:T(8,128)(2,1)S(1)} %reshape.19, bf16[]{:T(256)} %constant.2.clone.1), padding=0_0x0_4x0_48 | pad | bytes 186882 | tf_op jit(solution)/shard_map/jit(_pad)/pad | solution.py:457
  2.5 22.9 %shard_map.46 = f32[20,24,128]{2,1,0:T(8,128)} custom-call(bf16[20,24,128]{2,1,0:T(8,128)(2,1)} %pad.4.own, bf16[36,20,20]{2,1,0:T(8,128)(2,1)} %bitcast.11, bf16[36,20,20]{2,1,0:T(8,128)(2,1)} %bitcast.12, bf16[20,2,20]{2,1,0:T(2,128)(2,1)} %bitcast.13), custom_call_target="tpu_custom_call" | custom-call | tf_op jit(solution)/shard_map/pallas_call | solution.py:466
  25.4 1.3 %reshape.22 = f32[20,20,4,20]{3,2,1,0:T(4,128)S(1)} reshape(f32[20,20,80]{2,1,0:T(8,128)} %bitcast.10) | data formatting | bytes 256000 | tf_op jit(solution)/shard_map/reshape | solution.py:514
  26.7 0.1 copy.10
  26.8 1.1 %reshape.23 = f32[1,1,4,8000]{3,2,1,0:T(4,128)} reshape(f32[4,20,20,20]{3,2,1,0:T(8,128)S(1)} %bitcast.8) | data formatting | bytes 256000 | tf_op jit(solution)/shard_map/reshape | solution.py:515

commit v3 on v2

--- a/solution.py
+++ b/solution.py
@@ -85,7 +85,7 @@
     if count == 1:
         body(0, 0)
     else:
-        lax.fori_loop(0, count, body, 0)
+        lax.fori_loop(0, count, body, 0, unroll=2)
 
 
 def spread_eight(n, lanes, groups):
@@ -169,6 +169,83 @@
                 dst[t * deep + s, rows, :] = jnp.where(at < kappa, v, other).astype(BF)
 
 
+def tiles_of(base, rows, n):
+    return base // LANES, (base + rows * n - 1) // LANES
+
+
+def mirror(n):
+    r, c = grid2(LANES, LANES)
+    group, p = lax.div(c, ROW), lax.rem(c, ROW)
+    g, s = lax.div(p, 8), lax.rem(p, 8)
+    count = jnp.minimum(n - 8 * g, 8)
+    return one((s < count) & (r == group * ROW + 8 * g + count - 1 - s) & (group < 3))
+
+
+def skew(v, n):
+    v = pltpu.roll(v, 0, 1, stride=n // 2, stride_axis=0)
+    return pltpu.roll(v, 0, 1, stride=n - n // 2, stride_axis=0)
+
+
+def unflatten(raw, flat, own, boxes, n):
+    size = raw.shape[-1]
+    flat[:, size // LANES * LANES :] = jnp.zeros((boxes, flat.shape[1] - size // LANES * LANES), F32)
+    flat[:, :size] = raw[0, 0].astype(F32)
+    s, at = grid2(8, LANES)
+    offset = at + s * n
+    place = lax.rem(at + s * n, LANES)
+    below = [place < (z + 1) * n for z in range(boxes)]
+    for i in range(n):
+        rows = []
+        for g in range(ROW // 8):
+            base = (i * n + 8 * g + min(8, n - 8 * g) - 1) * n
+            t = (base - 7 * n) // LANES
+            c = base - t * LANES
+            v = None
+            for z in reversed(range(boxes)):
+
+                def tile(k):
+                    line = flat[z : z + 1, (t + k) * LANES : (t + k + 1) * LANES]
+                    return jnp.broadcast_to(line, (8, LANES))
+
+                w = jnp.where(offset >= c, tile(0), tile(1))
+                if c + n > 2 * LANES:
+                    w = jnp.where(offset >= c - LANES, w, tile(2))
+                w = pltpu.roll(w, (z * n - c) % LANES, 1)
+                v = w if v is None else jnp.where(below[z], w, v)
+            rows.append(skew(v, n))
+        own[i] = jnp.concatenate(rows, axis=0).astype(BF)
+
+
+def flatten(rows, out, boxes, n):
+    size = out.shape[-1]
+    s, at = grid2(8, LANES)
+    offset = at - s * n
+    total = [[None] * (-(-size // LANES)) for _ in range(boxes)]
+    for i in range(n):
+        for g in range(ROW // 8):
+            base = (i * n + 8 * g) * n
+            count = min(8, n - 8 * g)
+            first, last = base // LANES, (base + count * n - 1) // LANES
+            c = base - first * LANES
+            v = skew(rows(g, i), n)
+            turned = [pltpu.roll(v, (c - z * n) % LANES, 1) for z in range(boxes)]
+            for t in range(first, last + 1):
+                lo = c - (t - first) * LANES
+                keep = (offset >= lo) & (offset < lo + n)
+                if count < 8:
+                    keep = keep & (s < count)
+                for z in range(boxes):
+                    old = total[z][t]
+                    total[z][t] = jnp.where(keep, turned[z], 0.0 if old is None else old)
+        for t in range(len(total[0])):
+            if total[0][t] is not None and ((t + 1) * LANES <= (i + 1) * n * n or i == n - 1):
+                end = min((t + 1) * LANES, size)
+                for z in range(boxes):
+                    line = jnp.sum(total[z][t], axis=0, keepdims=True)
+                    out[0, 0, z : z + 1, t * LANES : end] = line[:, : end - t * LANES]
+                    total[z][t] = None
+
+
 def first_pass(u, rows, w, a, n, blocks):
     def body(p, carry):
         rhs = jnp.concatenate([u[2 * p, :rows, :], u[2 * p + 1, :rows, :]], axis=1)
@@ -180,7 +257,7 @@
             ).astype(BF)
         return carry
 
-    lax.fori_loop(0, n // 2, body, 0, unroll=5 if n % 10 == 0 else 1)
+    lax.fori_loop(0, n // 2, body, 0, unroll=True)
 
 
 def second_pass(fields, second, mid, n, terms, at):
@@ -196,7 +273,7 @@
             mid[m, g * n8 : (g + 1) * n8, at : at + LANES] = p[:, g * LANES : (g + 1) * LANES]
         return carry
 
-    lax.fori_loop(0, terms, body, 0, unroll=4 if terms % 4 == 0 else 1)
+    lax.fori_loop(0, terms, body, 0, unroll=True)
 
 
 def third_pass(mid, third, terms):
@@ -204,11 +281,18 @@
 
 
 def kernel(
+    raw_hbm,
+    fine_hbm,
+    coarse_hbm,
+    filt_hbm,
+    out,
+    raw,
+    filt,
     own,
+    flat,
     fine_blk,
     coarse_blk,
-    filt,
-    out,
+    acc,
     opk,
     npk,
     u,
@@ -241,6 +325,7 @@
     precv,
     csend,
     crecv,
+    bsem,
     *,
     boxes,
     nx,
@@ -291,6 +376,14 @@
             device_id_type=MESH,
         )
 
+    fetch = [
+        pltpu.make_async_copy(raw_hbm, raw, bsem.at[2]),
+        pltpu.make_async_copy(filt_hbm, filt, bsem.at[3]),
+        pltpu.make_async_copy(fine_hbm, fine_blk, bsem.at[0]),
+        pltpu.make_async_copy(coarse_hbm, coarse_blk, bsem.at[1]),
+    ]
+    for f in fetch:
+        f.start()
     barrier = pltpu.get_barrier_semaphore()
     count = jnp.int32(0)
     for dx, dy, exists in near + far:
@@ -312,9 +405,12 @@
         def _():
             ppk[c, :, :n, :] = jnp.zeros((deep, n, LANES), BF)
 
+    fetch[0].wait()
+    unflatten(raw, flat, own, boxes, n)
     pack(own, opk, n, kappa)
 
     fpad[...] = jnp.zeros_like(fpad)
+    fetch[1].wait()
     for e in range(2):
         fpad[e, :n, :n] = filt[:, e, :].astype(F32)
     r, c = grid2(PAD, PAD)
@@ -324,7 +420,8 @@
     for e in range(2):
         tpad[e, :, :PAD] = dot_t(eye, mats[e])
     turned = [tpad[e][:, :PAD].astype(BF) for e in range(2)]
-    fy = fpad[py][:ROW, :ROW].astype(BF)
+    perm = mirror(n)
+    fy = dot(fpad[py][:ROW, :].astype(BF), perm)[:, :ROW].astype(BF)
     fx = fpad[px][:ROW, :].astype(BF)
     widen(fx, spread_eight(n, 2 * LANES, 1), wide, fsecond, n, 1, 2 * LANES)
     fz = pair_mats(mats, boxes, boxes // 2, n)
@@ -357,9 +454,11 @@
         part[:, g * 8 : (g + 1) * 8, :] = s.reshape(deep, 8, LANES).astype(BF)
     mate_copy(0).start()
 
+    fetch[2].wait()
     cats(fine_blk, pad, n, terms)
     build_first(pad, first, terms)
     build_second(first[...], second, wide, terms, n)
+    first[...] = dot(first[...], perm).astype(BF)
 
     mate_copy(0).wait_recv()
     half[:, :n, :] = (part[:, :n, :].astype(F32) + got[0, :, :n, :].astype(F32)).astype(BF)
@@ -378,6 +477,7 @@
         def _():
             far_copy(c).start()
 
+    fetch[3].wait()
     cats(coarse_blk, pad, n, terms)
     build_first(pad, first_c, terms)
     r, c = grid2(4 * ROW, 4 * ROW)
@@ -407,9 +507,7 @@
         unpack(npk.at[c], u, slice((c + 1) * ROW, (c + 2) * ROW), n, kappa)
     first_pass(u, 3 * ROW, first, a.at[0], n, terms * 3)
     second_pass([a.at[0], a.at[1], a.at[2]], second, mid, n, terms, 0)
-    o = third_pass(mid, third, terms)
-    for g in range(3):
-        out[:, g * 8 : (g + 1) * 8, :] = o[g * n8 : (g + 1) * n8].reshape(n, 8, LANES)
+    acc[...] = third_pass(mid, third, terms)
 
     unpack_parent(cpk, cu, slice(0, ROW), n, half_k, True)
     for c in range(4):
@@ -426,10 +524,8 @@
     first_pass(cx.at[1], ROW, first_c, a.at[2], n, terms * 3)
     first_pass(cu, 3 * ROW, first_c, a.at[0], n, terms * 3)
     second_pass([a.at[0], a.at[1], a.at[2]], second_c, mid_c, n, terms, 0)
-    o = third_pass(mid_c, third_c, terms)
-    for g in range(3):
-        at = slice(g * 8, (g + 1) * 8)
-        out[:, at, :] = out[:, at, :] + o[g * n8 : (g + 1) * n8].reshape(n, 8, LANES)
+    acc[...] += third_pass(mid_c, third_c, terms)
+    flatten(lambda g, i: acc[g * n8 + i * 8 : g * n8 + (i + 1) * 8, :], out, boxes, n)
 
     for c in range(2):
         mate_copy(c).wait_send()
@@ -445,6 +541,10 @@
 
 
 VM = pl.BlockSpec(memory_space=pltpu.VMEM)
+
+
+def in_hbm(x):
+    return pltpu.with_memory_space_constraint(x, pltpu.HBM)
 
 
 def shards(nx, ny, fine_source, fine_blocks, coarse_blocks, filters):
@@ -452,9 +552,6 @@
     terms, n = fine_blocks.shape[1], fine_blocks.shape[2]
     n8 = n * 8
     deep = (n + 2) // 3
-    raw = fine_source.reshape(boxes, n, n, n)
-    own = raw.transpose(1, 2, 0, 3).reshape(n, n, boxes * n)
-    own = jnp.pad(own, ((0, 0), (0, ROW - n), (0, LANES - boxes * n)))
     dma = pltpu.SemaphoreType.DMA
 
     def bf(*shape):
@@ -463,12 +560,19 @@
     def f32(*shape):
         return pltpu.VMEM(shape, F32)
 
-    out = pl.pallas_call(
+    return pl.pallas_call(
         functools.partial(kernel, boxes=boxes, nx=nx, ny=ny),
-        out_shape=jax.ShapeDtypeStruct((n, ROW, LANES), F32),
-        in_specs=[VM] * 4,
+        out_shape=jax.ShapeDtypeStruct(fine_source.shape, F32),
+        in_specs=[pl.BlockSpec(memory_space=pltpu.HBM)] * 4,
         out_specs=VM,
         scratch_shapes=[
+            bf(*fine_source.shape),
+            bf(n, 2, n),
+            bf(n, ROW, LANES),
+            f32(boxes, (fine_source.shape[3] // LANES + 3) * LANES),
+            bf(3 * terms, n, n),
+            bf(3 * terms, n, n),
+            f32(3 * n8, LANES),
             bf(2 * deep, ROW, LANES),
             bf(4, 2 * deep, ROW, LANES),
             bf(n, 3 * ROW, LANES),
@@ -501,18 +605,17 @@
             dma((2,)),
             dma((4,)),
             dma((4,)),
+            dma((4,)),
         ],
         compiler_params=pltpu.CompilerParams(
-            vmem_limit_bytes=60 * 1024 * 1024, collective_id=0, has_side_effects=True
+            vmem_limit_bytes=32 * 1024 * 1024, collective_id=0, has_side_effects=True
         ),
     )(
-        own,
-        fine_blocks.reshape(3 * terms, n, n),
-        coarse_blocks.reshape(3 * terms, n, n),
-        filters.transpose(1, 0, 2),
+        in_hbm(fine_source),
+        in_hbm(fine_blocks.reshape(3 * terms, n, n)),
+        in_hbm(coarse_blocks.reshape(3 * terms, n, n)),
+        in_hbm(filters.transpose(1, 0, 2)),
     )
-    out = out[:, :n, : boxes * n].reshape(n, n, boxes, n).transpose(2, 0, 1, 3)
-    return out.reshape(1, 1, boxes, n * n * n)
 
 
 def solution(mesh):

time: 28.1 us -> 23.7 us (0.84)
  local copies, waits for them, and re-layouts: 4.94 us -> 0.65 us
    reshape x5 -> x0, local copies, waits for them, and re-layouts: 4.05 us -> none  [the longest x2 1.39 us: shards(): out = out[:, :n, :boxes * n].reshape(n, n, boxes, n).transpose(2, 0, 1, 3)]
    pad x1 -> x0, local copies, waits for them, and re-layouts: 0.68 us -> none  [shards(): own = jnp.pad(own, ((0, 0), (0, ROW - n), (0, LANES - boxes * n)))]
    unnamed x0 -> x1, local copies, waits for them, and re-layouts: none -> 0.65 us
where the time goes in v3:
time: 23.7 us; the launch traced here: 23.5 us
  Pallas kernels  22.9 us (97%)
  local copies, waits for them, and re-layouts  0.65 us (3%)
    pallas_call x1, Pallas kernels, shards(): pl.pallas_call(functools.partial(kernel, boxes=boxes, nx=nx, ny=ny), out_...  22.9 us
    unnamed x1, local copies, waits for them, and re-layouts  0.65 us

profile of v3, /device:TPU:0, one launch (start us, length us, event | category | flops | bytes accessed | tf_op | source)
XLA Modules:
  0.0 23.5 jit_solution(2509508822599451018)
XLA Ops:
  0.0 22.9 %shard_map.46 = f32[1,1,4,8000]{3,2,1,0:T(4,128)S(1)} custom-call(bf16[1,1,4,8000]{3,2,1,0:T(4,128)(2,1)} %raw_hbm.1, bf16[36,20,20]{2,1,0:T(8,128)(2,1)} %bitcast.3, bf16[36,20,20]{2,1,0:T(8,128)(2,1)} %bitcast.4, bf16[20,2,20]{2,1,0:T(2,128)(2,1)} %bitcast.5), custom_call_target="tpu_custom_call" | custom-call | tf_op jit(solution)/shard_map/pallas_call | solution.py:563
  22.9 0.7 %copy.6 = f32[1,1,4,8000]{3,2,1,0:T(4,128)} copy(f32[1,1,4,8000]{3,2,1,0:T(4,128)S(1)} %shard_map.46) | data formatting | bytes 256000

commit v4 on v3

--- a/solution.py
+++ b/solution.py
@@ -98,26 +98,41 @@
     widen(source, spread_eight(n, 4 * LANES, 3), wide, second, n, terms, 4 * LANES)
 
 
-def build_third(pad, third, terms, boxes, n, grow):
+def build_third(pad, lines, third, terms, boxes, n, grow):
     both = grow is not None
-    wide = dot(pad[:, :PAD].astype(BF), repeat_lanes(PAD, n, boxes * n * (1 + both))).astype(BF)
-    left = repeat_rows(ROW, n, boxes * n)
-    r, c = grid2(LANES, LANES)
-    row, col = lax.div(r, n), lax.div(c, n)
-    side = col - boxes if both else col
+    lines[...] = dot(pad[:, :PAD].astype(BF), repeat_lanes(PAD, n, boxes * n * (1 + both)))
+    col = lax.div(grid2(ROW, LANES)[1], n)
+    spare = jnp.zeros((LANES - boxes * ROW, LANES), F32)
     for m in range(terms):
-        low, mid, up = (
-            dot(left, wide[(e * terms + m) * ROW : (e * terms + m + 1) * ROW]) for e in range(3)
-        )
-        main = jnp.where((row == col) & (col < boxes), mid, 0.0)
-        other = jnp.where(side == row + 1, up, 0.0)
-        other = other + jnp.where((side == row - 1) & (side >= 0), low, 0.0)
+        low, mid, up = three(lines, m, terms)
+        main, other = [], []
+        for z in range(boxes):
+            shift = boxes if both else 0
+            side = jnp.where(col == shift + z + 1, up, 0.0)
+            if z > 0:
+                side = jnp.where(col == shift + z - 1, low, side)
+            if both:
+                main.append(jnp.where(col == z, mid, side))
+            else:
+                main.append(jnp.where(col == z, mid, 0.0))
+                other.append(side)
         if both:
-            third[:, m * LANES : (m + 1) * LANES] = dot(grow, (main + other).astype(BF)).astype(BF)
+            tile = jnp.concatenate(main, axis=0).astype(BF)
+            third[:, m * LANES : (m + 1) * LANES] = dot(grow, tile).astype(BF)
         else:
             at = m * 2 * LANES
-            third[:, at : at + LANES] = main.astype(BF)
-            third[:, at + LANES : at + 2 * LANES] = other.astype(BF)
+            third[:, at : at + LANES] = jnp.concatenate(main + [spare], axis=0).astype(BF)
+            third[:, at + LANES : at + 2 * LANES] = jnp.concatenate(other + [spare], axis=0).astype(BF)
+
+
+def growth(tpad, boxes):
+    rows = [
+        tpad[e][:ROW] if z == 0 else pltpu.roll(tpad[e][:ROW], z * ROW, 1)
+        for z in range(boxes)
+        for e in range(2)
+    ]
+    rows.append(jnp.zeros((LANES - 2 * boxes * ROW, LANES), F32))
+    return jnp.concatenate(rows, axis=0).astype(BF)[:, : boxes * ROW]
 
 
 def pair_mats(mats, boxes_in, boxes_out, n):
@@ -228,7 +243,7 @@
             first, last = base // LANES, (base + count * n - 1) // LANES
             c = base - first * LANES
             v = skew(rows(g, i), n)
-            turned = [pltpu.roll(v, (c - z * n) % LANES, 1) for z in range(boxes)]
+            turned = [pltpu.roll(v, (c - z * ROW) % LANES, 1) for z in range(boxes)]
             for t in range(first, last + 1):
                 lo = c - (t - first) * LANES
                 keep = (offset >= lo) & (offset < lo + n)
@@ -293,6 +308,7 @@
     fine_blk,
     coarse_blk,
     acc,
+    lines,
     opk,
     npk,
     u,
@@ -406,11 +422,11 @@
             ppk[c, :, :n, :] = jnp.zeros((deep, n, LANES), BF)
 
     fetch[0].wait()
+    fetch[1].wait()
     unflatten(raw, flat, own, boxes, n)
     pack(own, opk, n, kappa)
 
     fpad[...] = jnp.zeros_like(fpad)
-    fetch[1].wait()
     for e in range(2):
         fpad[e, :n, :n] = filt[:, e, :].astype(F32)
     r, c = grid2(PAD, PAD)
@@ -419,7 +435,6 @@
     tpad[...] = jnp.zeros_like(tpad)
     for e in range(2):
         tpad[e, :, :PAD] = dot_t(eye, mats[e])
-    turned = [tpad[e][:, :PAD].astype(BF) for e in range(2)]
     perm = mirror(n)
     fy = dot(fpad[py][:ROW, :].astype(BF), perm)[:, :ROW].astype(BF)
     fx = fpad[px][:ROW, :].astype(BF)
@@ -464,18 +479,9 @@
     half[:, :n, :] = (part[:, :n, :].astype(F32) + got[0, :, :n, :].astype(F32)).astype(BF)
     mate_copy(1).start()
 
-    build_third(pad, third, terms, boxes, n, None)
+    build_third(pad, lines, third, terms, boxes, n, None)
     first_pass(own, ROW, first, a.at[3], n, terms * 3)
     second_pass([a.at[3]], second, mid, n, terms, LANES)
-
-    mate_copy(1).wait_recv()
-    cpk[:, n:, :] = jnp.zeros((deep, ROW - n, LANES), BF)
-    cpk[:, :n, :] = (half[:, :n, :].astype(F32) + got[1, :, :n, :].astype(F32)).astype(BF)
-    for c in range(4):
-
-        @pl.when(far[c][2])
-        def _():
-            far_copy(c).start()
 
     fetch[3].wait()
     cats(coarse_blk, pad, n, terms)
@@ -490,7 +496,7 @@
 
     build_second(grown(first_c, quad(tpad[px][:, :PAD].astype(BF)), terms), second_c, wide, terms, n)
     first_c[...] = grown(first_c, quad(tpad[py][:, :PAD].astype(BF)), terms)
-    build_third(pad, third_c, terms, boxes // 2, n, pair_mats(turned, boxes // 2, boxes, n).astype(BF))
+    build_third(pad, lines, third_c, terms, boxes // 2, n, growth(tpad, boxes // 2))
 
     def near_wait(c):
         @pl.when(near[c][2])
@@ -501,6 +507,15 @@
         near_wait(c)
         unpack(npk.at[c], ux.at[c - 2], slice(0, ROW), n, kappa)
         first_pass(ux.at[c - 2], ROW, first, a.at[c - 1], n, terms * 3)
+    mate_copy(1).wait_recv()
+    cpk[:, n:, :] = jnp.zeros((deep, ROW - n, LANES), BF)
+    cpk[:, :n, :] = (half[:, :n, :].astype(F32) + got[1, :, :n, :].astype(F32)).astype(BF)
+    for c in range(4):
+
+        @pl.when(far[c][2])
+        def _():
+            far_copy(c).start()
+
     u[:, :ROW, :] = own[...]
     for c in (0, 1):
         near_wait(c)
@@ -573,6 +588,7 @@
             bf(3 * terms, n, n),
             bf(3 * terms, n, n),
             f32(3 * n8, LANES),
+            f32(3 * terms * ROW, LANES),
             bf(2 * deep, ROW, LANES),
             bf(4, 2 * deep, ROW, LANES),
             bf(n, 3 * ROW, LANES),

time: 23.7 us -> 20.1 us (0.85)
  Pallas kernels: 22.9 us -> 19.3 us
    pallas_call x1, Pallas kernels: 22.9 us -> 19.3 us  [shards(): pl.pallas_call(functools.partial(kernel, boxes=boxes, nx=nx, ny=ny), out_...]
where the time goes in v4:
time: 20.1 us; the launch traced here: 20 us
  Pallas kernels  19.3 us (96%)
  local copies, waits for them, and re-layouts  0.65 us (3%)
    pallas_call x1, Pallas kernels, shards(): pl.pallas_call(functools.partial(kernel, boxes=boxes, nx=nx, ny=ny), out_...  19.3 us
    unnamed x1, local copies, waits for them, and re-layouts  0.65 us

profile of v4, /device:TPU:0, one launch (start us, length us, event | category | flops | bytes accessed | tf_op | source)
XLA Modules:
  0.0 20.0 jit_solution(3232050977670805780)
XLA Ops:
  0.0 19.3 %shard_map.46 = f32[1,1,4,8000]{3,2,1,0:T(4,128)S(1)} custom-call(bf16[1,1,4,8000]{3,2,1,0:T(4,128)(2,1)} %raw_hbm.1, bf16[36,20,20]{2,1,0:T(8,128)(2,1)} %bitcast.3, bf16[36,20,20]{2,1,0:T(8,128)(2,1)} %bitcast.4, bf16[20,2,20]{2,1,0:T(2,128)(2,1)} %bitcast.5), custom_call_target="tpu_custom_call" | custom-call | tf_op jit(solution)/shard_map/pallas_call | solution.py:578
  19.4 0.7 %copy.6 = f32[1,1,4,8000]{3,2,1,0:T(4,128)} copy(f32[1,1,4,8000]{3,2,1,0:T(4,128)S(1)} %shard_map.46) | data formatting | bytes 256000

commit v5 on v4

--- a/solution.py
+++ b/solution.py
@@ -100,7 +100,7 @@
 
 def build_third(pad, lines, third, terms, boxes, n, grow):
     both = grow is not None
-    lines[...] = dot(pad[:, :PAD].astype(BF), repeat_lanes(PAD, n, boxes * n * (1 + both)))
+    lines[...] = dot(pad[:, :PAD].astype(BF), repeat_lanes(PAD, n, boxes * n * (3 if both else 1)))
     col = lax.div(grid2(ROW, LANES)[1], n)
     spare = jnp.zeros((LANES - boxes * ROW, LANES), F32)
     for m in range(terms):
@@ -108,11 +108,11 @@
         main, other = [], []
         for z in range(boxes):
             shift = boxes if both else 0
-            side = jnp.where(col == shift + z + 1, up, 0.0)
+            side = jnp.where(col == shift + z + 1, up, 0.0) if z + 1 < boxes else jnp.zeros_like(up)
             if z > 0:
                 side = jnp.where(col == shift + z - 1, low, side)
             if both:
-                main.append(jnp.where(col == z, mid, side))
+                main.append(jnp.where((col == z) | (col == 2 * boxes + z), mid, side))
             else:
                 main.append(jnp.where(col == z, mid, 0.0))
                 other.append(side)
@@ -181,7 +181,22 @@
                 other = 0.0
                 if twice:
                     other = tile if t == 1 else pltpu.roll(tile, (LANES - (t - 1) * kappa) % LANES, 1)
+                if twice:
+                    other = jnp.where(at < 2 * kappa, other, 0.0)
                 dst[t * deep + s, rows, :] = jnp.where(at < kappa, v, other).astype(BF)
+
+
+def unpack_sides(plus, minus, dst, n, kappa):
+    at = lane((ROW, LANES))
+    deep = (n + 2) // 3
+    for s in range(deep):
+        up, low = plus[s].astype(F32), minus[s].astype(F32)
+        for t in range(3):
+            if t * deep + s < n:
+                v = up if t == 0 else pltpu.roll(up, LANES - t * kappa, 1)
+                w = low if t == 2 else pltpu.roll(low, (2 - t) * kappa, 1)
+                w = jnp.where((at >= 2 * kappa) & (at < 3 * kappa), w, 0.0)
+                dst[t * deep + s] = jnp.where(at < kappa, v, w).astype(BF)
 
 
 def tiles_of(base, rows, n):
@@ -273,6 +288,17 @@
         return carry
 
     lax.fori_loop(0, n // 2, body, 0, unroll=True)
+
+
+def first_pass_sides(u, w, a_up, a_low, n, blocks, kappa):
+    at = lane((16, LANES))
+    for p in range(n // 2):
+        o = dot(w[:, :ROW], jnp.concatenate([u[2 * p], u[2 * p + 1]], axis=1))
+        rows = slice(p * 16, (p + 1) * 16)
+        for t in range(blocks):
+            v = jnp.concatenate([o[t * 8 : t * 8 + 8, :LANES], o[t * 8 : t * 8 + 8, LANES:]], axis=0)
+            a_up[t, rows, :] = jnp.where(at < kappa, v, 0.0).astype(BF)
+            a_low[t, rows, :] = jnp.where(at < kappa, 0.0, v).astype(BF)
 
 
 def second_pass(fields, second, mid, n, terms, at):
@@ -533,10 +559,8 @@
 
         if c < 2:
             unpack_parent(ppk.at[c], cu, slice((c + 1) * ROW, (c + 2) * ROW), n, half_k, False)
-        else:
-            unpack_parent(ppk.at[c], cx.at[c - 2], slice(0, ROW), n, half_k, False)
-    first_pass(cx.at[0], ROW, first_c, a.at[1], n, terms * 3)
-    first_pass(cx.at[1], ROW, first_c, a.at[2], n, terms * 3)
+    unpack_sides(ppk.at[2], ppk.at[3], cx, n, half_k)
+    first_pass_sides(cx, first_c, a.at[1], a.at[2], n, terms * 3, half_k)
     first_pass(cu, 3 * ROW, first_c, a.at[0], n, terms * 3)
     second_pass([a.at[0], a.at[1], a.at[2]], second_c, mid_c, n, terms, 0)
     acc[...] += third_pass(mid_c, third_c, terms)
@@ -599,7 +623,7 @@
             bf(deep, ROW, LANES),
             bf(4, deep, ROW, LANES),
             bf(n, 3 * ROW, LANES),
-            bf(2, n, ROW, LANES),
+            bf(n, ROW, LANES),
             f32(2, PAD, LANES),
             f32(2, PAD, LANES),
             f32(3 * terms * ROW, LANES),

time: 20.1 us -> 19.7 us (0.980)
  Pallas kernels: 19.3 us -> 18.9 us
    pallas_call x1, Pallas kernels: 19.3 us -> 18.9 us  [shards(): pl.pallas_call(functools.partial(kernel, boxes=boxes, nx=nx, ny=ny), out_...]
where the time goes in v5:
time: 19.7 us; the launch traced here: 19.6 us
  Pallas kernels  18.9 us (96%)
  local copies, waits for them, and re-layouts  0.65 us (3%)
    pallas_call x1, Pallas kernels, shards(): pl.pallas_call(functools.partial(kernel, boxes=boxes, nx=nx, ny=ny), out_...  18.9 us
    unnamed x1, local copies, waits for them, and re-layouts  0.65 us

profile of v5, /device:TPU:0, one launch (start us, length us, event | category | flops | bytes accessed | tf_op | source)
XLA Modules:
  0.0 19.6 jit_solution(1750431262531003178)
XLA Ops:
  0.0 18.9 %shard_map.46 = f32[1,1,4,8000]{3,2,1,0:T(4,128)S(1)} custom-call(bf16[1,1,4,8000]{3,2,1,0:T(4,128)(2,1)} %raw_hbm.1, bf16[36,20,20]{2,1,0:T(8,128)(2,1)} %bitcast.3, bf16[36,20,20]{2,1,0:T(8,128)(2,1)} %bitcast.4, bf16[20,2,20]{2,1,0:T(2,128)(2,1)} %bitcast.5), custom_call_target="tpu_custom_call" | custom-call | tf_op jit(solution)/shard_map/pallas_call | solution.py:602
  18.9 0.7 %copy.6 = f32[1,1,4,8000]{3,2,1,0:T(4,128)} copy(f32[1,1,4,8000]{3,2,1,0:T(4,128)S(1)} %shard_map.46) | data formatting | bytes 256000
